TPU v7x, 32 devices: a whole 2x2x4 slice. The times are simulated.
32 devices in a mesh: cluster: 8 (over z, y), sub: 4 (over x, core).
Axes of the slice: x: 2, y: 2, z: 4, core: 2. Of those that a mesh axis runs over, the one named last changes fastest.
Arguments:
- right_side: float32 [4, 8, 16, 384], P('sub', 'cluster'), may hold values from -12 to 12
- schur: float32 [4, 8, 768, 768], P('sub', 'cluster'), as said below
- rigid_modes: float32 [4, 8, 6, 768], P('sub', 'cluster'), may hold values from -0.21875 to 0.21875
- mode_count: int32 [4, 8], P('sub', 'cluster'), may hold values from 3 to 6
- face_order: int32 [4, 8, 384], P('sub', 'cluster'), may hold values from 0 to 383, each once within a row
- dual_scale: float32 [4, 8, 384], P('sub', 'cluster'), may hold values from 0.5 to 2
- rigid_loads: float32 [4, 8, 6, 16], P('sub', 'cluster'), may hold values from -6 to 6
- coarse_inverse: float32 [192, 192], P(('cluster', 'sub')), as said below
Outputs:
- multipliers: float32 [4, 8, 16, 384], P('sub', 'cluster')
- residual: float32 [4, 8, 16, 384], P('sub', 'cluster')
Inputs may be any that keep to these rules, and one draw needn't show every extreme that they name: rigid-body modes m with m >= mode_count are unused. `face_order`: each subdomain's entries form a permutation of the face unknowns; those of the first subdomain of a chain are unused. `schur`: each subdomain's matrix is symmetric. `coarse_inverse`: symmetric.
All inputs are finite; a program needn't handle non-finite values.
Results may differ from a plain program's by a relative error of at most 0.0003.
Values sent between devices are 32-bit elements; how exact they have to be, the bound alone decides.
No kernel may reach another device: no remote copies, remote signals or barrier semaphores. Data moves between devices by JAX's collectives and lax.ppermute only.
A program may use at most 64 MiB of HBM per device.

v0:
```python
import jax
import jax.numpy as jnp
from jax import lax
from jax.sharding import PartitionSpec as P

ITERS = 2


highest = lax.Precision.HIGHEST


def from_behind(block, axis, distance):
    devices = range(lax.axis_size(axis))
    route = [(i - distance, i) for i in devices if i - distance in devices]
    return lax.ppermute(block, axis, route)


def permute_faces(field, index):

    def single_face(values, order):
        return jnp.take(values, order, axis=1)

    return jax.vmap(jax.vmap(single_face))(field, index)


def lift_faces(dual_field, face_order):
    incoming = from_behind(dual_field, "cluster", 1)
    earlier = jnp.concatenate([incoming, dual_field[:, :-1]], axis=1)
    left_face = -permute_faces(earlier, face_order)
    return jnp.concatenate([left_face, dual_field], axis=3)


def push_faces(values, inverse):
    half_size = values.shape[3] // 2
    left_face = values[..., :half_size]
    right_face = values[..., half_size:]
    returned = -permute_faces(left_face, inverse)
    outgoing = from_behind(returned, "cluster", -1)
    following = jnp.concatenate([returned[:, 1:], outgoing], axis=1)
    return right_face + following


def apply_dual(dual_field, schur, face_order, inverse):
    lifted = lift_faces(dual_field, face_order)
    dual_image = jnp.einsum("sjci,sjik->sjck", lifted, schur, precision=highest)
    return push_faces(dual_image, inverse)


def basis_transpose(dual_field, basis, face_order):
    return jnp.einsum(
        "sjmi,sjci->sjmc", basis, lift_faces(dual_field, face_order), precision=highest
    )


def basis_expand(coefficients, basis, inverse):
    return push_faces(
        jnp.einsum("sjmi,sjmc->sjci", basis, coefficients, precision=highest), inverse
    )


def coarse_plain(coefficients, coarse_rows):
    flattened = coefficients.reshape(-1, coefficients.shape[3])
    solved = lax.psum_scatter(
        jnp.dot(coarse_rows.T, flattened, precision=highest),
        ("cluster", "sub"),
        scatter_dimension=0,
        tiled=True,
    )
    return solved.reshape(coefficients.shape)


def project(dual_field, basis, face_order, inverse, coarse_rows):
    coefficients = basis_transpose(dual_field, basis, face_order)
    return dual_field - basis_expand(coarse_plain(coefficients, coarse_rows), basis, inverse)


def gram_product(first_field, second_field):
    return jnp.einsum("sjcm,sjdm->cd", first_field, second_field, precision=highest)


def solve_small(matrix, right_hand):
    factor = jnp.linalg.cholesky(matrix)
    halfway = lax.linalg.triangular_solve(factor, right_hand, left_side=True, lower=True)
    return lax.linalg.triangular_solve(
        factor, halfway, left_side=True, lower=True, transpose_a=True
    )


def step_quantities(dual_image, direction, residual, basis, face_order, inverse, coarse_rows):
    curvature_part = gram_product(direction, dual_image)
    descent_part = gram_product(direction, residual)
    coefficients = basis_transpose(dual_image, basis, face_order)
    curvature, descent = lax.psum((curvature_part, descent_part), ("cluster", "sub"))
    solved = coarse_plain(coefficients, coarse_rows)
    projected_image = dual_image - basis_expand(solved, basis, inverse)
    return (curvature, descent, projected_image)


def shards(
    right_side, schur, rigid_modes, mode_count, face_order, dual_scale, rigid_loads, coarse_inverse
):
    inverse = jnp.argsort(face_order, axis=-1)
    active = (jnp.arange(rigid_modes.shape[2])[None, None, :] < mode_count[:, :, None]).astype(
        jnp.float32
    )
    basis = rigid_modes * active[..., None]
    masked_loads = rigid_loads * active[..., None]
    scaling = dual_scale[:, :, None, :]
    multipliers = basis_expand(coarse_plain(masked_loads, coarse_inverse), basis, inverse)
    residual = project(
        right_side - apply_dual(multipliers, schur, face_order, inverse),
        basis,
        face_order,
        inverse,
        coarse_inverse,
    )
    search = project(scaling * residual, basis, face_order, inverse, coarse_inverse)
    direction = search
    for iteration in range(ITERS):
        dual_image = apply_dual(direction, schur, face_order, inverse)
        curvature, descent, projected_image = step_quantities(
            dual_image, direction, residual, basis, face_order, inverse, coarse_inverse
        )
        step_size = solve_small(curvature, descent)
        multipliers = multipliers + jnp.einsum(
            "sjcm,cd->sjdm", direction, step_size, precision=highest
        )
        residual = residual - jnp.einsum(
            "sjcm,cd->sjdm", projected_image, step_size, precision=highest
        )
        if iteration + 1 < ITERS:
            search = project(scaling * residual, basis, face_order, inverse, coarse_inverse)
            update = lax.psum(gram_product(dual_image, search), ("cluster", "sub"))
            correction = -solve_small(curvature, update)
            direction = search + jnp.einsum(
                "sjcm,cd->sjdm", direction, correction, precision=highest
            )
    return (multipliers, residual)


def solution(mesh):
    in_specs = (
        P("sub", "cluster", None, None),
        P("sub", "cluster", None, None),
        P("sub", "cluster", None, None),
        P("sub", "cluster"),
        P("sub", "cluster", None),
        P("sub", "cluster", None),
        P("sub", "cluster", None, None),
        P(("cluster", "sub"), None),
    )
    out_specs = (P("sub", "cluster", None, None), P("sub", "cluster", None, None))
    return jax.shard_map(shards, mesh=mesh, in_specs=in_specs, out_specs=out_specs, check_vma=False)
```

profile of v0, /device:TPU:0, one launch (start us, length us, event | category | flops | bytes accessed | tf_op | source)
XLA Modules:
  0.0 494.8 jit_solution(11295149442735976061)
XLA Ops:
  9.6 42.1 %all-reduce = f32[192,16]{0,1:T(8,128)S(1)} all-reduce(f32[192,16]{0,1:T(8,128)S(1)} %convolution_bitcast_fusion.16), channel_id=2, replica_groups=mesh['cluster'=8,'sub'=4] {'cluster','sub'}, use_global_device_ids=true, to_apply=%region_0.0.clone | all-reduce | flops 3072 | bytes 24576
  60.3 4.0 collective-permute-done
  64.3 4.8 collective-permute-start.1
  81.4 4.7 collective-permute-done.2
  86.1 4.8 collective-permute-start.3
  92.6 3.8 gather_fusion.3
  96.9 40.7 %all-reduce.1 = f32[192,16]{0,1:T(8,128)S(1)} all-reduce(f32[192,16]{0,1:T(8,128)S(1)} %convolution_bitcast_fusion.15), channel_id=3, replica_groups=mesh['cluster'=8,'sub'=4] {'cluster','sub'}, use_global_device_ids=true, to_apply=%region_2.4.clone | all-reduce | flops 3072 | bytes 24576
  138.0 3.8 gather_fusion.4
  143.3 4.7 collective-permute-done.4
  148.0 4.8 collective-permute-start.5
  154.4 3.8 gather_fusion.5
  158.8 40.0 %all-reduce.2 = f32[192,16]{0,1:T(8,128)S(1)} all-reduce(f32[192,16]{0,1:T(8,128)S(1)} %convolution_bitcast_fusion.14), channel_id=4, replica_groups=mesh['cluster'=8,'sub'=4] {'cluster','sub'}, use_global_device_ids=true, to_apply=%region_3.5.clone | all-reduce | flops 3072 | bytes 24576
  204.4 4.7 collective-permute-done.6
  209.2 5.0 %collective-permute-start.7 = (f32[1,1,16,384]{3,2,1,0:T(8,128)S(1)}, f32[1,1,16,384]{3,2,1,0:T(8,128)S(1)}, u32[]{:S(2)}, u32[]{:S(2)}) collective-permute-start(f32[1,1,16,384]{3,2,1,0:T(8,128)S(1)} %fusion.48), channel_id=1, source_target_pairs={{0,4},{4,8},{8,12},{12,16},{16,20},{20,24},{24,28},{1,5},{5,9},{9,... | collective-permute-start | bytes 73736 | tf_op jit(solution)/shard_map/ppermute | solution.py:15
  215.6 3.8 gather_fusion.7
  226.3 4.6 collective-permute-done.8
  230.9 4.8 collective-permute-start.9
  241.7 40.3 %all-reduce.7 = (f32[16,16]{1,0:T(8,128)S(1)}, f32[16,16]{0,1:T(8,128)S(1)}, f32[192,16]{0,1:T(8,128)S(1)}) all-reduce(f32[16,16]{1,0:T(8,128)S(1)} %fusion.99, f32[16,16]{0,1:T(8,128)S(1)} %fusion.102, f32[192,16]{0,1:T(8,128)S(1)} %convolution_bitcast_fusion.13), channel_id=1, replica_groups=mesh['cluster'=8,'sub'=4] {'cluster','sub'}, use_global_device_ids=true, to_apply=%region_7.10 | all-reduce | flops 3584 | bytes 28672 | tf_op jit(solution)/shard_map/psum | solution.py:93
  292.1 4.4 collective-permute-done.10
  296.7 5.0 %collective-permute-start.11 = (f32[1,1,16,384]{3,2,1,0:T(8,128)S(1)}, f32[1,1,16,384]{3,2,1,0:T(8,128)S(1)}, u32[]{:S(2)}, u32[]{:S(2)}) collective-permute-start(f32[1,1,16,384]{3,2,1,0:T(8,128)S(1)} %get-tuple-element.18), channel_id=1, source_target_pairs={{0,4},{4,8},{8,12},{12,16},{16,20},{20,24},{24,28},{1,5},{5,9},{9,... | collective-permute-start | bytes 73736 | tf_op jit(solution)/shard_map/ppermute | solution.py:15
  303.2 3.8 gather_fusion.11
  307.5 40.1 %all-reduce.4 = f32[192,16]{0,1:T(8,128)S(1)} all-reduce(f32[192,16]{0,1:T(8,128)S(1)} %convolution_bitcast_fusion.12), channel_id=6, replica_groups=mesh['cluster'=8,'sub'=4] {'cluster','sub'}, use_global_device_ids=true, to_apply=%region_9.0.clone | all-reduce | flops 3072 | bytes 24576
  353.3 4.7 collective-permute-done.12
  358.1 40.7 %psum.37 = f32[16,16]{1,0:T(8,128)S(1)} all-reduce(f32[16,16]{1,0:T(8,128)S(1)} %fusion.97), channel_id=1, replica_groups=mesh['cluster'=8,'sub'=4] {'cluster','sub'}, use_global_device_ids=true, to_apply=%region_10.0 | all-reduce | flops 256 | bytes 2048 | tf_op jit(solution)/shard_map/psum | solution.py:133
  399.4 4.2 collective-permute-start.13
  405.2 3.8 gather_fusion.13
  410.5 3.8 gather_fusion.14
  415.9 4.6 collective-permute-done.14
  420.5 5.1 %collective-permute-start.15 = (f32[1,1,16,384]{3,2,1,0:T(8,128)S(1)}, f32[1,1,16,384]{3,2,1,0:T(8,128)S(1)}, u32[]{:S(2)}, u32[]{:S(2)}) collective-permute-start(f32[1,1,16,384]{3,2,1,0:T(8,128)S(1)} %slice_add_fusion.1), channel_id=1, source_target_pairs={{0,4},{4,8},{8,12},{12,16},{16,20},{20,24},{24,28},{1,5},{5,9},{9,... | collective-permute-start | bytes 73736 | tf_op jit(solution)/shard_map/ppermute | solution.py:15
  426.9 3.8 gather_fusion.15
  431.3 40.4 %all-reduce.6 = (f32[16,16]{1,0:T(8,128)S(1)}, f32[16,16]{0,1:T(8,128)S(1)}, f32[192,16]{0,1:T(8,128)S(1)}) all-reduce(f32[16,16]{1,0:T(8,128)S(1)} %fusion.90, f32[16,16]{0,1:T(8,128)S(1)} %fusion.92, f32[192,16]{0,1:T(8,128)S(1)} %convolution_bitcast_fusion.11), channel_id=1, replica_groups=mesh['cluster'=8,'sub'=4] {'cluster','sub'}, use_global_device_ids=true, to_apply=%region_12.0 | all-reduce | flops 3584 | bytes 28672 | tf_op jit(solution)/shard_map/psum | solution.py:93
  476.7 3.8 gather_fusion.16
  (164 shorter events, 85.3 us)
Async XLA Ops:
  7.2 67.6 %copy-start = (f32[1,1,768,768]{3,2,1,0:T(8,128)S(1)}, f32[1,1,768,768]{3,2,1,0:T(8,128)}, u32[]{:S(2)}) copy-start(f32[1,1,768,768]{3,2,1,0:T(8,128)} %param.16) | copy-start | bytes 7077892
  7.2 45.7 %sort.19.cloned.1.call-start = ((), (), s32[]{:S(2)}) async-start(), calls=%async_computation | async-start | bytes 9248 | tf_op jit(solution)/shard_map/jit(argsort)/sort | solution.py:102
  58.2 27.9 %copy-start.2 = (f32[1,1,16,384]{3,2,1,0:T(8,128)S(1)}, f32[1,1,16,384]{3,2,1,0:T(8,128)}, u32[]{:S(2)}) copy-start(f32[1,1,16,384]{3,2,1,0:T(8,128)} %param.15) | copy-start | bytes 73732
  58.3 6.0 %collective-permute-start = (f32[1,1,16,384]{3,2,1,0:T(8,128)S(1)}, f32[1,1,16,384]{3,2,1,0:T(8,128)S(1)}, u32[]{:S(2)}, u32[]{:S(2)}) collective-permute-start(f32[1,1,16,384]{3,2,1,0:T(8,128)S(1)} %fusion.89), channel_id=1, source_target_pairs={{4,0},{8,4},{12,8},{16,12},{20,16},{24,20},{28,24},{5,1},{9,5},{13... | collective-permute-start | bytes 73736 | tf_op jit(solution)/shard_map/ppermute | solution.py:15
  64.3 6.3 %collective-permute-start.1 = (f32[1,1,16,384]{3,2,1,0:T(8,128)S(1)}, f32[1,1,16,384]{3,2,1,0:T(8,128)S(1)}, u32[]{:S(2)}, u32[]{:S(2)}) collective-permute-start(f32[1,1,16,384]{3,2,1,0:T(8,128)S(1)} %slice_add_fusion.8), channel_id=1, source_target_pairs={{0,4},{4,8},{8,12},{12,16},{16,20},{20,24},{24,28},{1,5},{5,9},{9,... | collective-permute-start | bytes 73736 | tf_op jit(solution)/shard_map/ppermute | solution.py:15
  74.6 22.1 %copy-start.1 = (f32[6,192]{1,0:T(8,128)S(1)}, f32[6,192]{1,0:T(8,128)}, u32[]{:S(2)}) copy-start(f32[6,192]{1,0:T(8,128)} %param.22) | copy-start | bytes 13828
  74.7 68.5 %copy-start.3 = (f32[1,1,384]{2,1,0:T(1,128)S(1)}, f32[1,1,384]{2,1,0:T(1,128)}, u32[]{:S(2)}) copy-start(f32[1,1,384]{2,1,0:T(1,128)} %param.20) | copy-start | bytes 4612
  80.1 6.0 %collective-permute-start.2 = (f32[1,1,16,384]{3,2,1,0:T(8,128)S(1)}, f32[1,1,16,384]{3,2,1,0:T(8,128)S(1)}, u32[]{:S(2)}, u32[]{:S(2)}) collective-permute-start(f32[1,1,16,384]{3,2,1,0:T(8,128)S(1)} %fusion.87), channel_id=1, source_target_pairs={{4,0},{8,4},{12,8},{16,12},{20,16},{24,20},{28,24},{5,1},{9,5},{13... | collective-permute-start | bytes 73736 | tf_op jit(solution)/shard_map/ppermute | solution.py:15
  86.1 6.3 %collective-permute-start.3 = (f32[1,1,16,384]{3,2,1,0:T(8,128)S(1)}, f32[1,1,16,384]{3,2,1,0:T(8,128)S(1)}, u32[]{:S(2)}, u32[]{:S(2)}) collective-permute-start(f32[1,1,16,384]{3,2,1,0:T(8,128)S(1)} %fusion.50), channel_id=1, source_target_pairs={{0,4},{4,8},{8,12},{12,16},{16,20},{20,24},{24,28},{1,5},{5,9},{9,... | collective-permute-start | bytes 73736 | tf_op jit(solution)/shard_map/ppermute | solution.py:15
  141.9 6.0 %collective-permute-start.4 = (f32[1,1,16,384]{3,2,1,0:T(8,128)S(1)}, f32[1,1,16,384]{3,2,1,0:T(8,128)S(1)}, u32[]{:S(2)}, u32[]{:S(2)}) collective-permute-start(f32[1,1,16,384]{3,2,1,0:T(8,128)S(1)} %fusion.85), channel_id=1, source_target_pairs={{4,0},{8,4},{12,8},{16,12},{20,16},{24,20},{28,24},{5,1},{9,5},{13... | collective-permute-start | bytes 73736 | tf_op jit(solution)/shard_map/ppermute | solution.py:15
  148.0 6.3 %collective-permute-start.5 = (f32[1,1,16,384]{3,2,1,0:T(8,128)S(1)}, f32[1,1,16,384]{3,2,1,0:T(8,128)S(1)}, u32[]{:S(2)}, u32[]{:S(2)}) collective-permute-start(f32[1,1,16,384]{3,2,1,0:T(8,128)S(1)} %get-tuple-element.14), channel_id=1, source_target_pairs={{0,4},{4,8},{8,12},{12,16},{16,20},{20,24},{24,28},{1,5},{5,9},{9,... | collective-permute-start | bytes 73736 | tf_op jit(solution)/shard_map/ppermute | solution.py:15
  203.1 6.0 %collective-permute-start.6 = (f32[1,1,16,384]{3,2,1,0:T(8,128)S(1)}, f32[1,1,16,384]{3,2,1,0:T(8,128)S(1)}, u32[]{:S(2)}, u32[]{:S(2)}) collective-permute-start(f32[1,1,16,384]{3,2,1,0:T(8,128)S(1)} %fusion.83), channel_id=1, source_target_pairs={{4,0},{8,4},{12,8},{16,12},{20,16},{24,20},{28,24},{5,1},{9,5},{13... | collective-permute-start | bytes 73736 | tf_op jit(solution)/shard_map/ppermute | solution.py:15
  209.2 6.3 %collective-permute-start.7 = (f32[1,1,16,384]{3,2,1,0:T(8,128)S(1)}, f32[1,1,16,384]{3,2,1,0:T(8,128)S(1)}, u32[]{:S(2)}, u32[]{:S(2)}) collective-permute-start(f32[1,1,16,384]{3,2,1,0:T(8,128)S(1)} %fusion.48), channel_id=1, source_target_pairs={{0,4},{4,8},{8,12},{12,16},{16,20},{20,24},{24,28},{1,5},{5,9},{9,... | collective-permute-start | bytes 73736 | tf_op jit(solution)/shard_map/ppermute | solution.py:15
  224.9 6.0 %collective-permute-start.8 = (f32[1,1,16,384]{3,2,1,0:T(8,128)S(1)}, f32[1,1,16,384]{3,2,1,0:T(8,128)S(1)}, u32[]{:S(2)}, u32[]{:S(2)}) collective-permute-start(f32[1,1,16,384]{3,2,1,0:T(8,128)S(1)} %fusion.81), channel_id=1, source_target_pairs={{4,0},{8,4},{12,8},{16,12},{20,16},{24,20},{28,24},{5,1},{9,5},{13... | collective-permute-start | bytes 73736 | tf_op jit(solution)/shard_map/ppermute | solution.py:15
  230.9 6.3 %collective-permute-start.9 = (f32[1,1,16,384]{3,2,1,0:T(8,128)S(1)}, f32[1,1,16,384]{3,2,1,0:T(8,128)S(1)}, u32[]{:S(2)}, u32[]{:S(2)}) collective-permute-start(f32[1,1,16,384]{3,2,1,0:T(8,128)S(1)} %slice_add_fusion.4), channel_id=1, source_target_pairs={{0,4},{4,8},{8,12},{12,16},{16,20},{20,24},{24,28},{1,5},{5,9},{9,... | collective-permute-start | bytes 73736 | tf_op jit(solution)/shard_map/ppermute | solution.py:15
  290.5 6.0 %collective-permute-start.10 = (f32[1,1,16,384]{3,2,1,0:T(8,128)S(1)}, f32[1,1,16,384]{3,2,1,0:T(8,128)S(1)}, u32[]{:S(2)}, u32[]{:S(2)}) collective-permute-start(f32[1,1,16,384]{3,2,1,0:T(8,128)S(1)} %fusion.79), channel_id=1, source_target_pairs={{4,0},{8,4},{12,8},{16,12},{20,16},{24,20},{28,24},{5,1},{9,5},{13... | collective-permute-start | bytes 73736 | tf_op jit(solution)/shard_map/ppermute | solution.py:15
  296.7 6.3 %collective-permute-start.11 = (f32[1,1,16,384]{3,2,1,0:T(8,128)S(1)}, f32[1,1,16,384]{3,2,1,0:T(8,128)S(1)}, u32[]{:S(2)}, u32[]{:S(2)}) collective-permute-start(f32[1,1,16,384]{3,2,1,0:T(8,128)S(1)} %get-tuple-element.18), channel_id=1, source_target_pairs={{0,4},{4,8},{8,12},{12,16},{16,20},{20,24},{24,28},{1,5},{5,9},{9,... | collective-permute-start | bytes 73736 | tf_op jit(solution)/shard_map/ppermute | solution.py:15
  352.0 6.0 %collective-permute-start.12 = (f32[1,1,16,384]{3,2,1,0:T(8,128)S(1)}, f32[1,1,16,384]{3,2,1,0:T(8,128)S(1)}, u32[]{:S(2)}, u32[]{:S(2)}) collective-permute-start(f32[1,1,16,384]{3,2,1,0:T(8,128)S(1)} %fusion.77), channel_id=1, source_target_pairs={{4,0},{8,4},{12,8},{16,12},{20,16},{24,20},{28,24},{5,1},{9,5},{13... | collective-permute-start | bytes 73736 | tf_op jit(solution)/shard_map/ppermute | solution.py:15
  399.4 5.7 %collective-permute-start.13 = (f32[1,1,16,384]{3,2,1,0:T(8,128)S(1)}, f32[1,1,16,384]{3,2,1,0:T(8,128)S(1)}, u32[]{:S(2)}, u32[]{:S(2)}) collective-permute-start(f32[1,1,16,384]{3,2,1,0:T(8,128)S(1)} %fusion.18), channel_id=1, source_target_pairs={{0,4},{4,8},{8,12},{12,16},{16,20},{20,24},{24,28},{1,5},{5,9},{9,... | collective-permute-start | bytes 73736 | tf_op jit(solution)/shard_map/ppermute | solution.py:15
  414.5 6.0 %collective-permute-start.14 = (f32[1,1,16,384]{3,2,1,0:T(8,128)S(1)}, f32[1,1,16,384]{3,2,1,0:T(8,128)S(1)}, u32[]{:S(2)}, u32[]{:S(2)}) collective-permute-start(f32[1,1,16,384]{3,2,1,0:T(8,128)S(1)} %fusion.75), channel_id=1, source_target_pairs={{4,0},{8,4},{12,8},{16,12},{20,16},{24,20},{28,24},{5,1},{9,5},{13... | collective-permute-start | bytes 73736 | tf_op jit(solution)/shard_map/ppermute | solution.py:15
  420.5 6.3 %collective-permute-start.15 = (f32[1,1,16,384]{3,2,1,0:T(8,128)S(1)}, f32[1,1,16,384]{3,2,1,0:T(8,128)S(1)}, u32[]{:S(2)}, u32[]{:S(2)}) collective-permute-start(f32[1,1,16,384]{3,2,1,0:T(8,128)S(1)} %slice_add_fusion.1), channel_id=1, source_target_pairs={{0,4},{4,8},{8,12},{12,16},{16,20},{20,24},{24,28},{1,5},{5,9},{9,... | collective-permute-start | bytes 73736 | tf_op jit(solution)/shard_map/ppermute | solution.py:15
  480.7 6.0 %collective-permute-start.16 = (f32[1,1,16,384]{3,2,1,0:T(8,128)S(1)}, f32[1,1,16,384]{3,2,1,0:T(8,128)S(1)}, u32[]{:S(2)}, u32[]{:S(2)}) collective-permute-start(f32[1,1,16,384]{3,2,1,0:T(8,128)S(1)} %fusion.73), channel_id=1, source_target_pairs={{4,0},{8,4},{12,8},{16,12},{20,16},{24,20},{28,24},{5,1},{9,5},{13... | collective-permute-start | bytes 73736 | tf_op jit(solution)/shard_map/ppermute | solution.py:15
Sparse Core Ops, SparseCore 0:
  10.9 2.7 sort.21.cloned.1.call-done
  (1 shorter events, 0.0 us)
where the time goes:
time: 504 us; the launch traced here: 495 us
  blocking collectives  284 us (56%)
  local copies, waits for them, and re-layouts  69.8 us (14%)
  waiting for transfers between devices  51.2 us (10%)
  starting transfers between devices  50.3 us (10%)
  between operations  15.9 us (3%)
  matrix products  12.3 us (2%)
  other arithmetic  11.2 us (2%)
    unnamed x4, blocking collectives  163 us
    psum x2, blocking collectives, step_quantities(): lax.psum((curvature_part, descent_part), ('cluster', 'sub'))  80.7 us
    gather x34, local copies, waits for them, and re-layouts, single_face(): return jnp.take(values, order, axis=1)  66.8 us
    ppermute x17, waiting for transfers between devices, from_behind(): return lax.ppermute(block, axis, route)  51.2 us
    ppermute x17, starting transfers between devices, from_behind(): return lax.ppermute(block, axis, route)  50.3 us
    psum x1, blocking collectives, shards(): update = lax.psum(gram_product(dual_image, search), ('cluster', 'sub'))  40.7 us
  transfers between devices with their start and end apart: 17, of which 17 were waited for; matrix products, arithmetic and copies ran while one was open for 1% of the time, Pallas kernels for 0%

commit v1 on v0

v1 whole, which is shorter than its diff:
```python
import functools
import jax
import jax.numpy as jnp
from jax import lax
from jax.experimental import pallas as pl
from jax.experimental.pallas import tpu as pltpu
from jax.sharding import PartitionSpec as P

AXES = ("cluster", "sub")
f32 = jnp.float32
bf16 = jnp.bfloat16
PAD = 8


def dot(a, b, ca, cb):
    return lax.dot_general(
        a, b, (((ca,), (cb,)), ((), ())), precision=lax.Precision.HIGHEST, preferred_element_type=f32
    )


def nn(a, b):
    return dot(a, b, 1, 0)


def nt(a, b):
    return dot(a, b, 1, 1)


def tn(a, b):
    return dot(a, b, 0, 0)


def bdot(a, b, ca, cb):
    return lax.dot_general(a, b, (((ca,), (cb,)), ((), ())), preferred_element_type=f32)


def halves(x):
    high = x.astype(bf16)
    return high, (x - high.astype(f32)).astype(bf16)


def times_schur(x, high_ref, low_ref):
    rows = x.shape[0]
    xh, xl = halves(x)
    both = bdot(jnp.concatenate([xh, xl], axis=0), high_ref[...], 1, 0)
    return both[:rows] + both[rows:] + bdot(xh, low_ref[...], 1, 0)


def permuted_exact(x, one_hot):
    x1 = x.astype(bf16)
    rest = x - x1.astype(f32)
    x2 = rest.astype(bf16)
    x3 = (rest - x2.astype(f32)).astype(bf16)
    return bdot(x1, one_hot, 1, 1) + bdot(x2, one_hot, 1, 1) + bdot(x3, one_hot, 1, 1)


def prepare_kernel(
    schur, modes, count, order, later, load, coarse, rhs, scale,
    high, low, basis, to_right, to_left, payload,
):
    face = order.shape[1]
    k = modes.shape[0]
    cases = rhs.shape[0]
    nc = coarse.shape[1]
    hit = lax.broadcasted_iota(jnp.int32, (face, face), 0) == order[...]
    one_hot = jnp.where(hit, -1.0 * later[0].astype(f32), 0.0).astype(bf16)
    sh, sl = halves(schur[...])
    for part, out in ((sh, high), (sl, low)):
        top = bdot(one_hot, part[:face], 1, 0).astype(bf16)
        out[:face, :face] = bdot(top[:, :face], one_hot, 1, 1).astype(bf16)
        out[:face, face:] = top[:, face:]
        out[face:, :face] = bdot(part[face:, :face], one_hot, 1, 1).astype(bf16)
        out[face:, face:] = part[face:, face:]
    used = lax.broadcasted_iota(jnp.int32, (k, 1), 0) < count[0]
    masked = jnp.where(used, modes[...], 0.0)
    left = permuted_exact(masked[:, :face], one_hot)
    basis[...] = jnp.zeros_like(basis)
    basis[:k, :face] = left
    basis[:k, face:] = masked[:, face:]
    to_left[...] = jnp.zeros_like(to_left)
    to_left[:k] = left
    to_right[...] = jnp.zeros_like(to_right)
    to_right[:k] = masked[:, face:]
    to_right[PAD : PAD + cases] = rhs[...]
    to_right[PAD + cases : PAD + cases + 1] = scale[...]
    payload[...] = jnp.zeros_like(payload)
    peers = payload.shape[0]
    payload[:, :k, :nc] = jnp.broadcast_to(coarse[...][None], (peers, k, nc))
    payload[:, :k, nc : nc + cases] = jnp.broadcast_to(
        jnp.where(used, load[...], 0.0)[None], (peers, k, cases)
    )


def coarse_times(rows_ref, nc, values, packed, k):
    for i in range(nc // k):
        packed[i * k : (i + 1) * k] = values[i * PAD : i * PAD + k]
    return nn(rows_ref[:, :nc], packed[...])


def near_blocks(values, padded, here, stride):
    rows = values.shape[0]
    padded[:stride] = jnp.zeros((stride, values.shape[1]), f32)
    padded[stride + rows :] = jnp.zeros((stride, values.shape[1]), f32)
    padded[stride : stride + rows] = values
    start = here * PAD
    return jnp.concatenate(
        [padded[pl.ds(pl.multiple_of(start + b * stride, PAD), PAD), :] for b in range(3)], axis=0
    )


def gather_sum(wide, first, cases, stride):
    part = [wide[:, first + b * cases : first + (b + 1) * cases] for b in range(3)]
    none = jnp.zeros((stride, cases), f32)
    return (
        part[1]
        + jnp.concatenate([part[0][stride:], none], axis=0)
        + jnp.concatenate([none, part[2][:-stride]], axis=0)
    )


def scaled_gram_times(wide, first, values, k, near):
    rows, cases = values.shape
    blocks = rows // PAD
    matrix = wide[:, first : first + 3 * PAD].reshape(blocks, PAD, 3 * PAD)
    vector = values.reshape(blocks, PAD, cases)
    none = jnp.zeros((near, PAD, cases), f32)
    moved = [
        jnp.concatenate([none, vector[:-near]], axis=0),
        vector,
        jnp.concatenate([vector[near:], none], axis=0),
    ]
    total = jnp.zeros((blocks, PAD, cases), f32)
    for b in range(3):
        for m in range(k):
            total = total + matrix[:, :, b * PAD + m : b * PAD + m + 1] * moved[b][:, m : m + 1, :]
    return total.reshape(rows, cases)


def side_by_side(tall, blocks):
    return [tall[b * PAD : (b + 1) * PAD] for b in range(blocks)]


def start_kernel(
    here, gathered, high, low, basis, from_left, from_right, rhs, scale,
    frame, lifted_rhs, lifted_scale, start, v_left, v_right, payload, packed, padded, *, stride, k,
):
    face = rhs.shape[1]
    cases = rhs.shape[0]
    nc = packed.shape[0]
    y = coarse_times(gathered, nc, gathered[:, nc : nc + cases], packed, k)
    near = near_blocks(y, padded, here[0], stride)
    zero = jnp.zeros((PAD, face), f32)
    v = jnp.concatenate(
        [
            jnp.concatenate([from_left[:PAD], zero], axis=1),
            basis[...],
            jnp.concatenate([zero, from_right[...]], axis=1),
        ],
        axis=0,
    )
    frame[...] = v
    lb = jnp.concatenate([from_left[PAD : PAD + cases], rhs[...]], axis=1)
    ld = jnp.concatenate([from_left[PAD + cases : PAD + cases + 1], scale[...]], axis=1)
    lifted_rhs[...] = lb
    lifted_scale[...] = ld
    m0 = tn(near, v)
    start[...] = m0[:, face:]
    image = times_schur(m0, high, low)
    v_left[...] = image[:, :face]
    v_right[...] = image[:, face:]
    both = jnp.concatenate([v, v * ld], axis=0)
    shares = -nt(both, image)
    own = nt(jnp.concatenate([basis[...], basis[...] * ld], axis=0), lb)
    scaled = nt(basis[...] * ld, v)
    part = side_by_side(shares, 6)
    part[1] = part[1] + own[:PAD]
    part[4] = part[4] + own[PAD:]
    used = 6 * cases + 3 * PAD
    width = payload.shape[2]
    row = jnp.concatenate(part + [scaled, jnp.zeros((PAD, width - used), f32)], axis=1)
    payload[...] = jnp.broadcast_to(row[None], payload.shape)


def direction_kernel(
    here, gathered, coarse, high, low, frame, lifted_rhs, lifted_scale, m_left, m_right,
    from_left, from_right,
    search, residual, v_left, v_right, payload, packed, padded, *, stride, k,
):
    cases, face = m_left.shape
    nc = packed.shape[0]
    wide = gathered[...]
    g = gather_sum(wide, 0, cases, stride)
    h = gather_sum(wide, 3 * cases, cases, stride)
    c1 = coarse_times(coarse, nc, g, packed, k)
    c2 = coarse_times(
        coarse, nc, h - scaled_gram_times(wide, 6 * cases, c1, k, stride // PAD), packed, k
    )
    near1 = near_blocks(c1, padded, here[0], stride)
    near2 = near_blocks(c2, padded, here[0], stride)
    moved = jnp.concatenate([m_left[...] + from_left[...], m_right[...] + from_right[...]], axis=1)
    v = frame[...]
    r = lifted_rhs[...] - moved - tn(near1, v)
    s = lifted_scale[...] * r - tn(near2, v)
    search[...] = s
    residual[...] = r[:, face:]
    image = times_schur(s, high, low)
    v_left[...] = image[:, :face]
    v_right[...] = image[:, face:]
    shares = nt(jnp.concatenate([v, v * lifted_scale[...]], axis=0), image)
    energy = nt(s, image)
    part = side_by_side(shares, 6) + side_by_side(energy, cases // PAD)
    used = (6 + cases // PAD) * cases
    width = payload.shape[2]
    if width > used:
        part = part + [jnp.zeros((PAD, width - used), f32)]
    payload[...] = jnp.broadcast_to(jnp.concatenate(part, axis=1)[None], payload.shape)


def second_kernel(
    here, gathered, scaled, coarse, high, low, frame, lifted_scale, search, residual,
    s_left, s_right, from_left, from_right,
    projected, second, v_left, v_right, curvature, payload, packed, padded, *, stride, k,
):
    cases, face = s_left.shape
    nc = packed.shape[0]
    wide = gathered[...]
    g = gather_sum(wide, 0, cases, stride)
    h = gather_sum(wide, 3 * cases, cases, stride)
    for b in range(cases // PAD):
        piece = wide[:, (6 + b) * cases : (7 + b) * cases]
        curvature[b * PAD : (b + 1) * PAD] = piece.reshape(-1, PAD, cases).sum(axis=0)
    c1 = coarse_times(coarse, nc, g, packed, k)
    c2 = coarse_times(
        coarse, nc, h - scaled_gram_times(scaled[...], 6 * cases, c1, k, stride // PAD), packed, k
    )
    near1 = near_blocks(c1, padded, here[0], stride)
    near2 = near_blocks(c2, padded, here[0], stride)
    q = jnp.concatenate([s_left[...] + from_left[...], s_right[...] + from_right[...]], axis=1)
    v = frame[...]
    p = q - tn(near1, v)
    z = lifted_scale[...] * p - tn(near2, v)
    projected[...] = p[:, face:]
    zr = z[:, face:]
    second[...] = zr
    image = times_schur(z, high, low)
    v_left[...] = image[:, :face]
    v_right[...] = image[:, face:]
    r = residual[...]
    grams = nt(
        jnp.concatenate([search[:, face:], zr], axis=0),
        jnp.concatenate([r, p[:, face:], q[:, face:]], axis=0),
    )
    energy = nt(z, image)
    shares = side_by_side(nt(v, image), 3)
    top, bottom = grams[:cases], grams[cases:]
    crossed = nt(q[:, face:], zr)
    extra_top = jnp.concatenate(shares[:2], axis=1)
    extra_low = jnp.concatenate([shares[2], jnp.zeros((PAD, cases), f32)], axis=1)
    extra = jnp.concatenate([extra_top, extra_low], axis=0)
    row = [top[:, : 2 * cases], crossed, bottom[:, : 2 * cases], energy, extra]
    used = 8 * cases
    width = payload.shape[2]
    if width > used:
        row = row + [jnp.zeros((cases, width - used), f32)]
    payload[...] = jnp.broadcast_to(jnp.concatenate(row, axis=1)[None], payload.shape)


def eliminate(matrix, right):
    n = matrix.shape[0]
    work = jnp.concatenate([matrix, right], axis=1)
    rows = lax.broadcasted_iota(jnp.int32, work.shape, 0)
    for i in range(n):
        row = work[i : i + 1] / work[i : i + 1, i : i + 1]
        work = jnp.where(rows == i, row, work - work[:, i : i + 1] * row)
    return work[:, n:]


def finish_kernel(
    here, gathered, coarse, frame, start, search, residual, projected, second, curvature,
    v_right, from_right, out_mult, out_res, packed, *, stride, k, near,
):
    cases, face = start.shape
    nc = packed.shape[0]
    all_of = gathered[...]
    peers = all_of.shape[0]
    total = all_of.sum(axis=0)
    block = [total[:, b * cases : (b + 1) * cases] for b in range(6)]
    sr, sp, qz, zr, zp, zw = block
    low, mid = 6 * cases, 7 * cases
    part = [all_of[:, :PAD, low:mid], all_of[:, :PAD, mid : mid + cases], all_of[:, PAD : 2 * PAD, low:mid]]
    none = jnp.zeros((near, PAD, cases), f32)
    g = (
        part[1]
        + jnp.concatenate([part[0][near:], none], axis=0)
        + jnp.concatenate([none, part[2][:-near]], axis=0)
    ).reshape(peers * PAD, cases)
    for i in range(nc // k):
        packed[i * k : (i + 1) * k] = g[i * PAD : i * PAD + k]
    row = pl.multiple_of(here[0] * PAD, PAD)
    after = pl.multiple_of(here[1] * PAD, PAD)
    rows = jnp.concatenate([coarse[pl.ds(row, PAD), :nc], coarse[pl.ds(after, PAD), :nc]], axis=0)
    coefficients = nn(rows, packed[...])
    frame_right = frame[PAD : 3 * PAD, face:]
    w = v_right[...] + from_right[...] - tn(coefficients, frame_right)
    w0 = curvature[...]
    solved = eliminate(w0, jnp.concatenate([sr, qz], axis=1))
    a0, y = solved[:, :cases], solved[:, cases:]
    x = nn(y, a0)
    w1 = tn(a0, nn(zw, a0) - tn(qz, x))
    e1 = tn(x, sr - nn(sp, a0)) - tn(a0, zr - nn(zp, a0))
    a1 = eliminate(w1, e1)
    first = a0 + nn(x, a1)
    last = nn(a0, a1)
    out_mult[...] = start[...] + tn(first, search[:, face:]) - tn(last, second[...])
    out_res[...] = residual[...] - tn(first, projected[...]) + tn(last, w)


VMEM = pl.BlockSpec(memory_space=pltpu.VMEM)
SMEM = pl.BlockSpec(memory_space=pltpu.SMEM)


def call(kernel, args, outs, scratch, name, scalars):
    return pl.pallas_call(
        kernel,
        out_shape=[jax.ShapeDtypeStruct(s, d) for s, d in outs],
        in_specs=[SMEM if i in scalars else VMEM for i in range(len(args))],
        out_specs=[VMEM] * len(outs),
        scratch_shapes=[pltpu.VMEM(s, f32) for s in scratch],
        name=name,
    )(*args)


def exchange(to_right, to_left):
    n = lax.axis_size("cluster")
    from_left = lax.ppermute(to_right, "cluster", [(i, i + 1) for i in range(n - 1)])
    from_right = lax.ppermute(to_left, "cluster", [(i + 1, i) for i in range(n - 1)])
    return from_left, from_right


def spread(payload):
    return lax.all_to_all(payload, AXES, 0, 0)


def up(value, unit):
    return -(-value // unit) * unit


def shards(rhs, schur, modes, count, order, scale, load, coarse):
    chain = lax.axis_size("cluster")
    subs = lax.axis_size("sub")
    peers = chain * subs
    cases, face = rhs.shape[2:]
    size = schur.shape[2]
    k = modes.shape[2]
    nc = coarse.shape[1]
    stride = subs * PAD
    rows = peers * PAD
    at = lax.axis_index("cluster")
    me = at * subs + lax.axis_index("sub")
    here = jnp.stack([me, jnp.minimum(me + subs, peers - 1)]).astype(jnp.int32)
    later = (at > 0).astype(jnp.int32).reshape(1)
    rhs, schur, modes, load = rhs[0, 0], schur[0, 0], modes[0, 0], load[0, 0]
    count = count.reshape(1)
    order = order.reshape(1, face)
    scale = scale.reshape(1, face)
    vec = (cases, face)
    wide0 = up(nc + cases, 128)
    wide1 = up(6 * cases + 3 * PAD, 128)
    wide2 = up((6 + cases // PAD) * cases, 128)
    wide3 = up(8 * cases, 128)
    work = [(nc, cases), (rows + 2 * stride, cases)]
    head = functools.partial
    packet = up(PAD + cases + 1, 8)

    high, low, basis, to_right, to_left, payload = call(
        prepare_kernel,
        (schur, modes, count, order, later, load, coarse, rhs, scale),
        [
            ((size, size), bf16), ((size, size), bf16), ((PAD, size), f32),
            ((packet, face), f32), ((PAD, face), f32), ((peers, PAD, wide0), f32),
        ],
        [],
        "prepare",
        (2, 4),
    )
    from_left, from_right = exchange(to_right, to_left)
    coarse_rows = spread(payload).reshape(rows, wide0)

    frame, lifted_rhs, lifted_scale, start, m_left, m_right, payload = call(
        head(start_kernel, stride=stride, k=k),
        (here, coarse_rows, high, low, basis, from_left, from_right, rhs, scale),
        [
            ((3 * PAD, size), f32), ((cases, size), f32), ((1, size), f32), (vec, f32),
            (vec, f32), (vec, f32), ((peers, PAD, wide1), f32),
        ],
        work,
        "start",
        (0,),
    )
    from_left, from_right = exchange(m_right, m_left)
    first = spread(payload).reshape(rows, wide1)

    search, residual, s_left, s_right, payload = call(
        head(direction_kernel, stride=stride, k=k),
        (here, first, coarse_rows, high, low, frame, lifted_rhs, lifted_scale, m_left, m_right,
         from_left, from_right),
        [((cases, size), f32), (vec, f32), (vec, f32), (vec, f32), ((peers, PAD, wide2), f32)],
        work,
        "direction",
        (0,),
    )
    from_left, from_right = exchange(s_right, s_left)
    shared = spread(payload).reshape(rows, wide2)

    projected, second, z_left, z_right, curvature, payload = call(
        head(second_kernel, stride=stride, k=k),
        (here, shared, first, coarse_rows, high, low, frame, lifted_scale, search, residual,
         s_left, s_right, from_left, from_right),
        [(vec, f32), (vec, f32), (vec, f32), (vec, f32), ((cases, cases), f32),
         ((peers, cases, wide3), f32)],
        work,
        "second",
        (0,),
    )
    from_right = lax.ppermute(z_left, "cluster", [(i + 1, i) for i in range(chain - 1)])
    shared = spread(payload)

    multipliers, residual = call(
        head(finish_kernel, stride=stride, k=k, near=subs),
        (here, shared, coarse_rows, frame, start, search, residual, projected, second, curvature,
         z_right, from_right),
        [(vec, f32), (vec, f32)],
        [(nc, cases)],
        "finish",
        (0,),
    )
    return multipliers[None, None], residual[None, None]


def solution(mesh):
    in_specs = (
        P("sub", "cluster", None, None),
        P("sub", "cluster", None, None),
        P("sub", "cluster", None, None),
        P("sub", "cluster"),
        P("sub", "cluster", None),
        P("sub", "cluster", None),
        P("sub", "cluster", None, None),
        P(("cluster", "sub"), None),
    )
    out_specs = (P("sub", "cluster", None, None), P("sub", "cluster", None, None))
    return jax.shard_map(shards, mesh=mesh, in_specs=in_specs, out_specs=out_specs, check_vma=False)
```

time: 504 us -> 97.5 us (0.19); the launches traced: 495 us -> 96.7 us
  blocking collectives: 284 us -> 0 us
  local copies, waits for them, and re-layouts: 69.8 us -> 5.33 us
  waiting for transfers between devices: 51.2 us -> 18 us
  Pallas kernels: 0 us -> 26.6 us
  between operations: 15.9 us -> 1.4 us
  matrix products: 12.3 us -> 0 us
  other arithmetic: 11.2 us -> 0.61 us
  starting transfers between devices: 50.3 us -> 44.7 us
    unnamed x4 -> x0, blocking collectives: 163 us -> none
    psum x3 -> x0, blocking collectives: 121 us -> none  [the longest x2 80.7 us: step_quantities(): lax.psum((curvature_part, descent_part), ('cluster', 'sub'))]
    gather x34 -> x0, local copies, waits for them, and re-layouts: 66.8 us -> none  [single_face(): return jnp.take(values, order, axis=1)]
    ppermute x17 -> x7, waiting for transfers between devices: 51.2 us -> 9.56 us  [the longest x1 4.72 us: shards(): lax.ppermute(z_left, 'cluster', [(i + 1, i) for i in range(chain - 1)])]
    ppermute x17 -> x7, starting transfers between devices: 50.3 us -> 18.8 us  [the longest x3 13.6 us: exchange(): lax.ppermute(to_right, 'cluster', [(i, i + 1) for i in range(n - 1)])]
    pallas_call x0 -> x5, Pallas kernels: none -> 26.6 us  [call(): pl.pallas_call(kernel, out_shape=[jax.ShapeDtypeStruct(s, d) for s, d in...]
    all_to_all x0 -> x4, starting transfers between devices: none -> 25.9 us  [spread(): return lax.all_to_all(payload, AXES, 0, 0)]
    dot_general x30 -> x0, matrix products: 11.3 us -> none  [the longest x3 3.7 us: apply_dual(): dual_image = jnp.einsum('sjci,sjik->sjck', lifted, schur, precision=highest)]
  transfers between devices with their start and end apart: 17 -> 11, of which waited for: 17 -> 10; matrix products, arithmetic and copies ran while one was open for 1% -> 1% of each run, Pallas kernels for 0% -> 0%
where the time goes in v1:
time: 97.5 us; the launch traced here: 96.7 us
  starting transfers between devices  44.7 us (46%)
  Pallas kernels  26.6 us (27%)
  waiting for transfers between devices  18 us (18%)
  local copies, waits for them, and re-layouts  5.33 us (5%)
  between operations  1.4 us (1%)
    pallas_call x5, Pallas kernels, call(): pl.pallas_call(kernel, out_shape=[jax.ShapeDtypeStruct(s, d) for s, d in...  26.6 us
    all_to_all x4, starting transfers between devices, spread(): return lax.all_to_all(payload, AXES, 0, 0)  25.9 us
    ppermute x3, starting transfers between devices, exchange(): lax.ppermute(to_right, 'cluster', [(i, i + 1) for i in range(n - 1)])  13.6 us
    all_to_all x4, waiting for transfers between devices, spread(): return lax.all_to_all(payload, AXES, 0, 0)  8.49 us
    unnamed x24, local copies, waits for them, and re-layouts  5.33 us
    ppermute x1, waiting for transfers between devices, shards(): lax.ppermute(z_left, 'cluster', [(i + 1, i) for i in range(chain - 1)])  4.72 us
    ppermute x3, waiting for transfers between devices, exchange(): lax.ppermute(to_right, 'cluster', [(i, i + 1) for i in range(n - 1)])  4.41 us
    ppermute x3, starting transfers between devices, exchange(): lax.ppermute(to_left, 'cluster', [(i + 1, i) for i in range(n - 1)])  3.88 us
  transfers between devices with their start and end apart: 11, of which 10 were waited for; matrix products, arithmetic and copies ran while one was open for 1% of the time, Pallas kernels for 0%

profile of v1, /device:TPU:0, one launch (start us, length us, event | category | flops | bytes accessed | tf_op | source)
XLA Modules:
  0.0 96.7 jit_solution(10182021949518701528)
XLA Ops:
  1.3 1.3 %copy.15 = f32[1,1,6,16]{3,2,1,0:T(8,128)} copy(f32[1,1,6,16]{3,1,2,0:T(1,128)} %param.14) | data formatting | bytes 768
  2.6 1.3 %copy.14 = f32[1,1,6,768]{3,2,1,0:T(8,128)} copy(f32[1,1,6,768]{3,1,2,0:T(1,128)} %param.10) | data formatting | bytes 36864
  3.9 4.9 %prepare.1 = (bf16[768,768]{1,0:T(8,128)(2,1)}, bf16[768,768]{1,0:T(8,128)(2,1)}, f32[8,768]{1,0:T(8,128)}, f32[32,384]{1,0:T(8,128)}, f32[8,384]{1,0:T(8,128)}, /*index=5*/f32[32,8,256]{2,1,0:T(8,128)}) custom-call(f32[768,768]{1,0:T(8,128)} %bitcast.24, f32[6,768]{1,0:T(8,128)} %bitcast.30, s32[1]{0:T(128)} %bitcast.19.count, s32[1,384]{1,0:T(1,128)} %bitcast.34, ...), custom_call_target="tpu_custom_call" | custom-call | tf_op jit(solution)/shard_map/prepare/pallas_call | solution.py:323
  8.8 7.3 %all-to-all-start = ((f32[32,8,256]{2,1,0:T(8,128)}), f32[32,8,256]{2,1,0:T(8,128)S(1)}, u32[]{:S(2)}, u32[]{:S(2)}) async-start(f32[32,8,256]{2,1,0:T(8,128)} %get-tuple-element.28), calls=%async_computation | async-start | bytes 524288 | tf_op jit(solution)/shard_map/all_to_all | solution.py:341
  16.1 1.3 %collective-permute-start.1 = (f32[8,384]{1,0:T(8,128)}, f32[8,384]{1,0:T(8,128)S(1)}, u32[]{:S(2)}, u32[]{:S(2)}) collective-permute-start(f32[8,384]{1,0:T(8,128)} %get-tuple-element.33), channel_id=1, source_target_pairs={{4,0},{8,4},{12,8},{16,12},{20,16},{24,20},{28,24},{5,1},{9,5},{13... | collective-permute-start | bytes 36872 | tf_op jit(solution)/shard_map/ppermute | solution.py:336
  17.4 4.5 %collective-permute-start = (f32[32,384]{1,0:T(8,128)}, f32[32,384]{1,0:T(8,128)S(1)}, u32[]{:S(2)}, u32[]{:S(2)}) collective-permute-start(f32[32,384]{1,0:T(8,128)} %get-tuple-element.32), channel_id=1, source_target_pairs={{0,4},{4,8},{8,12},{12,16},{16,20},{20,24},{24,28},{1,5},{5,9},{9,... | collective-permute-start | bytes 147464 | tf_op jit(solution)/shard_map/ppermute | solution.py:335
  22.0 0.6 pad_add_fusion.here
  22.6 1.4 %collective-permute-done.from_left = f32[32,384]{1,0:T(8,128)S(1)} collective-permute-done((f32[32,384]{1,0:T(8,128)}, f32[32,384]{1,0:T(8,128)S(1)}, u32[]{:S(2)}, u32[]{:S(2)}) %collective-permute-start) | collective-permute-done | bytes 49184 | tf_op jit(solution)/shard_map/ppermute | solution.py:335
  24.1 2.7 %all-to-all-done = f32[32,8,256]{2,1,0:T(8,128)S(1)} async-done(((f32[32,8,256]{2,1,0:T(8,128)}), f32[32,8,256]{2,1,0:T(8,128)S(1)}, u32[]{:S(2)}, u32[]{:S(2)}) %all-to-all-start) | async-done | bytes 262176 | tf_op jit(solution)/shard_map/all_to_all | solution.py:341
  26.7 0.7 copy-done
  27.4 4.4 %start.1 = (f32[24,768]{1,0:T(8,128)}, f32[16,768]{1,0:T(8,128)}, f32[1,768]{1,0:T(1,128)}, f32[16,384]{1,0:T(8,128)}, f32[16,384]{1,0:T(8,128)}, /*index=5*/f32[16,384]{1,0:T(8,128)}, f32[32,8,128]{2,1,0:T(8,128)}) custom-call(s32[2]{0:T(128)} %pad_add_fusion.here, f32[256,256]{1,0:T(8,128)} %bitcast.20, bf16[768,768]{1,0:T(8,128)(2,1)} %get-tuple-element.29.high, ...), custom_call_target="tpu_custom_call" | custom-call | tf_op jit(solution)/shard_map/start/pallas_call | solution.py:323
  31.9 4.8 %all-to-all-start.1 = ((f32[32,8,128]{2,1,0:T(8,128)}), f32[32,8,128]{2,1,0:T(8,128)S(1)}, u32[]{:S(2)}, u32[]{:S(2)}) async-start(f32[32,8,128]{2,1,0:T(8,128)} %get-tuple-element.34), calls=%async_computation.1 | async-start | bytes 262144 | tf_op jit(solution)/shard_map/all_to_all | solution.py:341
  36.6 1.3 %collective-permute-start.3 = (f32[16,384]{1,0:T(8,128)}, f32[16,384]{1,0:T(8,128)S(1)}, u32[]{:S(2)}, u32[]{:S(2)}) collective-permute-start(f32[16,384]{1,0:T(8,128)} %get-tuple-element.38.m_left), channel_id=1, source_target_pairs={{4,0},{8,4},{12,8},{16,12},{20,16},{24,20},{28,24},{5,1},{9,5},{13... | collective-permute-start | bytes 73736 | tf_op jit(solution)/shard_map/ppermute | solution.py:336
  37.9 4.5 %collective-permute-start.2 = (f32[16,384]{1,0:T(8,128)}, f32[16,384]{1,0:T(8,128)S(1)}, u32[]{:S(2)}, u32[]{:S(2)}) collective-permute-start(f32[16,384]{1,0:T(8,128)} %get-tuple-element.39.m_right), channel_id=1, source_target_pairs={{0,4},{4,8},{8,12},{12,16},{16,20},{20,24},{24,28},{1,5},{5,9},{9,... | collective-permute-start | bytes 73736 | tf_op jit(solution)/shard_map/ppermute | solution.py:335
  42.7 1.5 %collective-permute-done.2.from_left = f32[16,384]{1,0:T(8,128)S(1)} collective-permute-done((f32[16,384]{1,0:T(8,128)}, f32[16,384]{1,0:T(8,128)S(1)}, u32[]{:S(2)}, u32[]{:S(2)}) %collective-permute-start.2) | collective-permute-done | bytes 24608 | tf_op jit(solution)/shard_map/ppermute | solution.py:335
  44.2 0.6 all-to-all-done.1
  44.9 0.7 copy-done.1
  45.5 5.5 %direction.1 = (f32[16,768]{1,0:T(8,128)}, f32[16,384]{1,0:T(8,128)}, f32[16,384]{1,0:T(8,128)}, f32[16,384]{1,0:T(8,128)}, f32[32,8,128]{2,1,0:T(8,128)}) custom-call(s32[2]{0:T(128)} %pad_add_fusion.here, f32[256,128]{1,0:T(8,128)} %bitcast.25, f32[256,256]{1,0:T(8,128)} %bitcast.21, bf16[768,768]{1,0:T(8,128)(2,1)} %get-tuple-element.29.high, ...), custom_call_target="tpu_custom_call" | custom-call | tf_op jit(solution)/shard_map/direction/pallas_call | solution.py:323
  51.0 6.9 %all-to-all-start.2 = ((f32[32,8,128]{2,1,0:T(8,128)}), f32[32,8,128]{2,1,0:T(8,128)S(1)}, u32[]{:S(2)}, u32[]{:S(2)}) async-start(f32[32,8,128]{2,1,0:T(8,128)} %get-tuple-element.40), calls=%async_computation.2 | async-start | bytes 262144 | tf_op jit(solution)/shard_map/all_to_all | solution.py:341
  57.9 1.3 %collective-permute-start.5 = (f32[16,384]{1,0:T(8,128)}, f32[16,384]{1,0:T(8,128)S(1)}, u32[]{:S(2)}, u32[]{:S(2)}) collective-permute-start(f32[16,384]{1,0:T(8,128)} %get-tuple-element.43.s_left), channel_id=1, source_target_pairs={{4,0},{8,4},{12,8},{16,12},{20,16},{24,20},{28,24},{5,1},{9,5},{13... | collective-permute-start | bytes 73736 | tf_op jit(solution)/shard_map/ppermute | solution.py:336
  59.2 4.5 %collective-permute-start.4 = (f32[16,384]{1,0:T(8,128)}, f32[16,384]{1,0:T(8,128)S(1)}, u32[]{:S(2)}, u32[]{:S(2)}) collective-permute-start(f32[16,384]{1,0:T(8,128)} %get-tuple-element.44.s_right), channel_id=1, source_target_pairs={{0,4},{4,8},{8,12},{12,16},{16,20},{20,24},{24,28},{1,5},{5,9},{9,... | collective-permute-start | bytes 73736 | tf_op jit(solution)/shard_map/ppermute | solution.py:335
  63.8 0.2 collective-permute-done.5.from_right
  64.0 1.5 %collective-permute-done.4.from_left = f32[16,384]{1,0:T(8,128)S(1)} collective-permute-done((f32[16,384]{1,0:T(8,128)}, f32[16,384]{1,0:T(8,128)S(1)}, u32[]{:S(2)}, u32[]{:S(2)}) %collective-permute-start.4) | collective-permute-done | bytes 24608 | tf_op jit(solution)/shard_map/ppermute | solution.py:335
  65.5 0.6 all-to-all-done.2
  66.1 0.6 copy-done.3
  66.8 5.5 %second.1 = (f32[16,384]{1,0:T(8,128)}, f32[16,384]{1,0:T(8,128)}, f32[16,384]{1,0:T(8,128)}, f32[16,384]{1,0:T(8,128)}, f32[16,16]{1,0:T(8,128)}, /*index=5*/f32[32,16,128]{2,1,0:T(8,128)}) custom-call(s32[2]{0:T(128)} %pad_add_fusion.here, f32[256,128]{1,0:T(8,128)} %bitcast.27, f32[256,128]{1,0:T(8,128)} %bitcast.26, f32[256,256]{1,0:T(8,128)} %bitcast.22, ...), custom_call_target="tpu_custom_call" | custom-call | tf_op jit(solution)/shard_map/second/pallas_call | solution.py:323
  72.3 6.9 %all-to-all-start.3 = ((f32[32,16,128]{2,1,0:T(8,128)}), f32[32,16,128]{2,1,0:T(8,128)S(1)}, u32[]{:S(2)}, u32[]{:S(2)}) async-start(f32[32,16,128]{2,1,0:T(8,128)} %get-tuple-element.45), calls=%async_computation.3 | async-start | bytes 524288 | tf_op jit(solution)/shard_map/all_to_all | solution.py:341
  79.2 1.3 %collective-permute-start.6 = (f32[16,384]{1,0:T(8,128)}, f32[16,384]{1,0:T(8,128)S(1)}, u32[]{:S(2)}, u32[]{:S(2)}) collective-permute-start(f32[16,384]{1,0:T(8,128)} %get-tuple-element.51), channel_id=1, source_target_pairs={{4,0},{8,4},{12,8},{16,12},{20,16},{24,20},{28,24},{5,1},{9,5},{13... | collective-permute-start | bytes 73736 | tf_op jit(solution)/shard_map/ppermute | solution.py:425
  80.5 4.7 %collective-permute-done.6.from_right = f32[16,384]{1,0:T(8,128)S(1)} collective-permute-done((f32[16,384]{1,0:T(8,128)}, f32[16,384]{1,0:T(8,128)S(1)}, u32[]{:S(2)}, u32[]{:S(2)}) %collective-permute-start.6) | collective-permute-done | bytes 24608 | tf_op jit(solution)/shard_map/ppermute | solution.py:425
  85.2 4.6 %all-to-all-done.3.gathered = f32[32,16,128]{2,1,0:T(8,128)S(1)} async-done(((f32[32,16,128]{2,1,0:T(8,128)}), f32[32,16,128]{2,1,0:T(8,128)S(1)}, u32[]{:S(2)}, u32[]{:S(2)}) %all-to-all-start.3) | async-done | bytes 262176 | tf_op jit(solution)/shard_map/all_to_all | solution.py:341
  89.8 0.7 copy-done.2
  90.5 6.2 %finish.1 = (f32[16,384]{1,0:T(8,128)}, f32[16,384]{1,0:T(8,128)}) custom-call(s32[2]{0:T(128)} %pad_add_fusion.here, f32[32,16,128]{2,1,0:T(8,128)} %copy-done.2, f32[256,256]{1,0:T(8,128)} %bitcast.23, f32[24,768]{1,0:T(8,128)} %get-tuple-element.35.frame, f32[16,384]{1,0:T(8,128)} %get-tuple-element.46.start, f32[16,768]{1,0:T(8,128)} %get-tuple-element.41.search, ...), custom_call_target="tpu_custom_call" | custom-call | tf_op jit(solution)/shard_map/finish/pallas_call | solution.py:323
  (20 shorter events, 0.2 us)
Async XLA Ops:
  8.8 17.9 %all-to-all-start = ((f32[32,8,256]{2,1,0:T(8,128)}), f32[32,8,256]{2,1,0:T(8,128)S(1)}, u32[]{:S(2)}, u32[]{:S(2)}) async-start(f32[32,8,256]{2,1,0:T(8,128)} %get-tuple-element.28), calls=%async_computation | async-start | bytes 524288 | tf_op jit(solution)/shard_map/all_to_all | solution.py:341
  16.1 6.5 %collective-permute-start.1 = (f32[8,384]{1,0:T(8,128)}, f32[8,384]{1,0:T(8,128)S(1)}, u32[]{:S(2)}, u32[]{:S(2)}) collective-permute-start(f32[8,384]{1,0:T(8,128)} %get-tuple-element.33), channel_id=1, source_target_pairs={{4,0},{8,4},{12,8},{16,12},{20,16},{24,20},{28,24},{5,1},{9,5},{13... | collective-permute-start | bytes 36872 | tf_op jit(solution)/shard_map/ppermute | solution.py:336
  17.4 6.6 %collective-permute-start = (f32[32,384]{1,0:T(8,128)}, f32[32,384]{1,0:T(8,128)S(1)}, u32[]{:S(2)}, u32[]{:S(2)}) collective-permute-start(f32[32,384]{1,0:T(8,128)} %get-tuple-element.32), channel_id=1, source_target_pairs={{0,4},{4,8},{8,12},{12,16},{16,20},{20,24},{24,28},{1,5},{5,9},{9,... | collective-permute-start | bytes 147464 | tf_op jit(solution)/shard_map/ppermute | solution.py:335
  22.6 4.1 %copy-start.10 = (f32[8,384]{1,0:T(8,128)}, f32[8,384]{1,0:T(8,128)S(1)}, u32[]{:S(2)}) copy-start(f32[8,384]{1,0:T(8,128)S(1)} %collective-permute-done.1.from_right) | copy-start | bytes 36868
  24.1 2.7 %copy-start.4 = (f32[32,384]{1,0:T(8,128)}, f32[32,384]{1,0:T(8,128)S(1)}, u32[]{:S(2)}) copy-start(f32[32,384]{1,0:T(8,128)S(1)} %collective-permute-done.from_left) | copy-start | bytes 147460
  26.7 0.7 copy-start
  31.9 13.0 %all-to-all-start.1 = ((f32[32,8,128]{2,1,0:T(8,128)}), f32[32,8,128]{2,1,0:T(8,128)S(1)}, u32[]{:S(2)}, u32[]{:S(2)}) async-start(f32[32,8,128]{2,1,0:T(8,128)} %get-tuple-element.34), calls=%async_computation.1 | async-start | bytes 262144 | tf_op jit(solution)/shard_map/all_to_all | solution.py:341
  36.6 6.1 %collective-permute-start.3 = (f32[16,384]{1,0:T(8,128)}, f32[16,384]{1,0:T(8,128)S(1)}, u32[]{:S(2)}, u32[]{:S(2)}) collective-permute-start(f32[16,384]{1,0:T(8,128)} %get-tuple-element.38.m_left), channel_id=1, source_target_pairs={{4,0},{8,4},{12,8},{16,12},{20,16},{24,20},{28,24},{5,1},{9,5},{13... | collective-permute-start | bytes 73736 | tf_op jit(solution)/shard_map/ppermute | solution.py:336
  37.9 6.3 %collective-permute-start.2 = (f32[16,384]{1,0:T(8,128)}, f32[16,384]{1,0:T(8,128)S(1)}, u32[]{:S(2)}, u32[]{:S(2)}) collective-permute-start(f32[16,384]{1,0:T(8,128)} %get-tuple-element.39.m_right), channel_id=1, source_target_pairs={{0,4},{4,8},{8,12},{12,16},{16,20},{20,24},{24,28},{1,5},{5,9},{9,... | collective-permute-start | bytes 73736 | tf_op jit(solution)/shard_map/ppermute | solution.py:335
  42.7 2.1 %copy-start.7 = (f32[16,384]{1,0:T(8,128)}, f32[16,384]{1,0:T(8,128)S(1)}, u32[]{:S(2)}) copy-start(f32[16,384]{1,0:T(8,128)S(1)} %collective-permute-done.3.from_right) | copy-start | bytes 73732
  44.2 0.6 copy-start.8
  44.8 0.7 copy-start.1
  51.0 15.1 %all-to-all-start.2 = ((f32[32,8,128]{2,1,0:T(8,128)}), f32[32,8,128]{2,1,0:T(8,128)S(1)}, u32[]{:S(2)}, u32[]{:S(2)}) async-start(f32[32,8,128]{2,1,0:T(8,128)} %get-tuple-element.40), calls=%async_computation.2 | async-start | bytes 262144 | tf_op jit(solution)/shard_map/all_to_all | solution.py:341
  57.9 6.1 %collective-permute-start.5 = (f32[16,384]{1,0:T(8,128)}, f32[16,384]{1,0:T(8,128)S(1)}, u32[]{:S(2)}, u32[]{:S(2)}) collective-permute-start(f32[16,384]{1,0:T(8,128)} %get-tuple-element.43.s_left), channel_id=1, source_target_pairs={{4,0},{8,4},{12,8},{16,12},{20,16},{24,20},{28,24},{5,1},{9,5},{13... | collective-permute-start | bytes 73736 | tf_op jit(solution)/shard_map/ppermute | solution.py:336
  59.2 6.3 %collective-permute-start.4 = (f32[16,384]{1,0:T(8,128)}, f32[16,384]{1,0:T(8,128)S(1)}, u32[]{:S(2)}, u32[]{:S(2)}) collective-permute-start(f32[16,384]{1,0:T(8,128)} %get-tuple-element.44.s_right), channel_id=1, source_target_pairs={{0,4},{4,8},{8,12},{12,16},{16,20},{20,24},{24,28},{1,5},{5,9},{9,... | collective-permute-start | bytes 73736 | tf_op jit(solution)/shard_map/ppermute | solution.py:335
  64.0 2.1 %copy-start.5 = (f32[16,384]{1,0:T(8,128)}, f32[16,384]{1,0:T(8,128)S(1)}, u32[]{:S(2)}) copy-start(f32[16,384]{1,0:T(8,128)S(1)} %collective-permute-done.5.from_right) | copy-start | bytes 73732
  65.5 0.6 copy-start.6
  66.1 0.6 copy-start.3
  72.3 17.5 %all-to-all-start.3 = ((f32[32,16,128]{2,1,0:T(8,128)}), f32[32,16,128]{2,1,0:T(8,128)S(1)}, u32[]{:S(2)}, u32[]{:S(2)}) async-start(f32[32,16,128]{2,1,0:T(8,128)} %get-tuple-element.45), calls=%async_computation.3 | async-start | bytes 524288 | tf_op jit(solution)/shard_map/all_to_all | solution.py:341
  79.2 6.0 %collective-permute-start.6 = (f32[16,384]{1,0:T(8,128)}, f32[16,384]{1,0:T(8,128)S(1)}, u32[]{:S(2)}, u32[]{:S(2)}) collective-permute-start(f32[16,384]{1,0:T(8,128)} %get-tuple-element.51), channel_id=1, source_target_pairs={{4,0},{8,4},{12,8},{16,12},{20,16},{24,20},{28,24},{5,1},{9,5},{13... | collective-permute-start | bytes 73736 | tf_op jit(solution)/shard_map/ppermute | solution.py:425
  85.2 4.6 %copy-start.9 = (f32[16,384]{1,0:T(8,128)}, f32[16,384]{1,0:T(8,128)S(1)}, u32[]{:S(2)}) copy-start(f32[16,384]{1,0:T(8,128)S(1)} %collective-permute-done.6.from_right) | copy-start | bytes 73732
  89.8 0.7 copy-start.2

commit v2 on v1

v2 whole, which is shorter than its diff:
```python
import functools
import math
import jax
import jax.numpy as jnp
from jax import lax
from jax.experimental import pallas as pl
from jax.experimental.pallas import tpu as pltpu
from jax.sharding import PartitionSpec as P

AXES = ("cluster", "sub")
f32 = jnp.float32
bf16 = jnp.bfloat16
PAD = 8


def dot(a, b, ca, cb):
    return lax.dot_general(
        a, b, (((ca,), (cb,)), ((), ())), precision=lax.Precision.HIGHEST, preferred_element_type=f32
    )


def nn(a, b):
    return dot(a, b, 1, 0)


def nt(a, b):
    return dot(a, b, 1, 1)


def tn(a, b):
    return dot(a, b, 0, 0)


def bdot(a, b, ca, cb):
    return lax.dot_general(a, b, (((ca,), (cb,)), ((), ())), preferred_element_type=f32)


def halves(x):
    high = x.astype(bf16)
    return high, (x - high.astype(f32)).astype(bf16)


def times_schur(x, high_ref, low_ref):
    rows = x.shape[0]
    xh, xl = halves(x)
    both = bdot(jnp.concatenate([xh, xl], axis=0), high_ref[...], 1, 0)
    return both[:rows] + both[rows:] + bdot(xh, low_ref[...], 1, 0)


def permuted_exact(x, one_hot):
    x1 = x.astype(bf16)
    rest = x - x1.astype(f32)
    x2 = rest.astype(bf16)
    x3 = (rest - x2.astype(f32)).astype(bf16)
    return bdot(x1, one_hot, 1, 1) + bdot(x2, one_hot, 1, 1) + bdot(x3, one_hot, 1, 1)


def split_sides(me, subs, right, left):
    even = (me // subs) % 2 == 0
    return jnp.where(even, right, left), jnp.where(even, left, right)


def join_sides(me, subs, chain, even_got, odd_got):
    at = me // subs
    even = at % 2 == 0
    left = jnp.where(even, odd_got, even_got)
    right = jnp.where(even, even_got, odd_got)
    return jnp.where(at > 0, left, 0.0), jnp.where(at < chain - 1, right, 0.0)


def signed_one_hot(me, subs, order):
    face = order.shape[1]
    hit = lax.broadcasted_iota(jnp.int32, (face, face), 0) == order
    sign = jnp.where(me // subs > 0, -1.0, 0.0)
    return jnp.where(hit, sign, 0.0).astype(bf16)


def pack_kernel(
    me, count, modes_in, order_in, load_in, coarse_in, rhs_in, scale_in,
    basis, own, to_even, to_odd, payload,
    modes, order, load, coarse, rhs, scale, sems, *, subs,
):
    pairs = (
        (order_in, order), (modes_in, modes), (coarse_in, coarse), (rhs_in, rhs),
        (scale_in, scale), (load_in, load),
    )
    copies = [pltpu.make_async_copy(a, b, sems.at[i]) for i, (a, b) in enumerate(pairs)]
    for copy in copies:
        copy.start()
    payload[...] = jnp.zeros_like(payload)
    own[...] = jnp.zeros_like(own)
    basis[...] = jnp.zeros_like(basis)
    face = order.shape[1]
    k = modes.shape[0]
    cases = rhs.shape[0]
    nc = coarse.shape[1]
    copies[0].wait()
    one_hot = signed_one_hot(me[0], subs, order[...])
    for copy in copies[1:]:
        copy.wait()
    used = lax.broadcasted_iota(jnp.int32, (k, 1), 0) < count[0]
    for i in range(k):
        basis[i : i + 1] = jnp.where(i < count[0], modes[i], 0.0)
    left = permuted_exact(basis[:, :face], one_hot)
    basis[:, :face] = left
    own[:PAD] = basis[:, face:]
    own[PAD : PAD + cases] = rhs[...]
    own[PAD + cases : PAD + cases + 1] = scale[...]
    rest = jnp.zeros((own.shape[0] - PAD, face), f32)
    to_even[...], to_odd[...] = split_sides(
        me[0], subs, own[...], jnp.concatenate([left, rest], axis=0)
    )
    peers = payload.shape[0]
    payload[:, :k, :nc] = jnp.broadcast_to(coarse[...][None], (peers, k, nc))
    for i in range(k):
        row = jnp.where(i < count[0], load[i], 0.0)
        payload[:, i : i + 1, nc : nc + cases] = jnp.broadcast_to(row[None], (peers, 1, cases))


def permute_kernel(me, order, schur, high, low, *, subs):
    face = order.shape[1]
    one_hot = signed_one_hot(me[0], subs, order[...])
    sh, sl = halves(schur[...])
    for part, out in ((sh, high), (sl, low)):
        top = bdot(one_hot, part[:face], 1, 0).astype(bf16)
        out[:face, :face] = bdot(top[:, :face], one_hot, 1, 1).astype(bf16)
        out[:face, face:] = top[:, face:]
        out[face:, :face] = bdot(part[face:, :face], one_hot, 1, 1).astype(bf16)
        out[face:, face:] = part[face:, face:]


def coarse_times(rows_ref, nc, values, packed, k):
    for i in range(nc // k):
        packed[i * k : (i + 1) * k] = values[i * PAD : i * PAD + k]
    return nn(rows_ref[:, :nc], packed[...])


def near_blocks(values, padded, here, stride):
    rows = values.shape[0]
    padded[:stride] = jnp.zeros((stride, values.shape[1]), f32)
    padded[stride + rows :] = jnp.zeros((stride, values.shape[1]), f32)
    padded[stride : stride + rows] = values
    start = here * PAD
    return jnp.concatenate(
        [padded[pl.ds(pl.multiple_of(start + b * stride, PAD), PAD), :] for b in range(3)], axis=0
    )


def gather_sum(wide, first, cases, stride):
    part = [wide[:, first + b * cases : first + (b + 1) * cases] for b in range(3)]
    none = jnp.zeros((stride, cases), f32)
    return (
        part[1]
        + jnp.concatenate([part[0][stride:], none], axis=0)
        + jnp.concatenate([none, part[2][:-stride]], axis=0)
    )


def scaled_gram_times(wide, first, values, k, near):
    rows, cases = values.shape
    blocks = rows // PAD
    matrix = wide[:, first : first + 3 * PAD].reshape(blocks, PAD, 3 * PAD)
    vector = values.reshape(blocks, PAD, cases)
    none = jnp.zeros((near, PAD, cases), f32)
    moved = [
        jnp.concatenate([none, vector[:-near]], axis=0),
        vector,
        jnp.concatenate([vector[near:], none], axis=0),
    ]
    total = jnp.zeros((blocks, PAD, cases), f32)
    for b in range(3):
        for m in range(k):
            total = total + matrix[:, :, b * PAD + m : b * PAD + m + 1] * moved[b][:, m : m + 1, :]
    return total.reshape(rows, cases)


def side_by_side(tall, blocks):
    return [tall[b * PAD : (b + 1) * PAD] for b in range(blocks)]


def load_kernel(me, gathered, near, packed, padded, *, stride, k):
    nc, cases = packed.shape
    y = coarse_times(gathered, nc, gathered[:, nc : nc + cases], packed, k)
    near[...] = near_blocks(y, padded, me[0], stride)


def start_kernel(
    me, near, high, low, basis, own, even_got, odd_got,
    frame, lifted_rhs, lifted_scale, start, image_out, to_even, to_odd, payload, *, subs, chain,
):
    face = own.shape[1]
    cases = near.shape[1]
    from_left, from_right = join_sides(me[0], subs, chain, even_got[...], odd_got[...])
    zero = jnp.zeros((PAD, face), f32)
    v = jnp.concatenate(
        [
            jnp.concatenate([from_left[:PAD], zero], axis=1),
            basis[...],
            jnp.concatenate([zero, from_right[:PAD]], axis=1),
        ],
        axis=0,
    )
    frame[...] = v
    both = jnp.concatenate([from_left, own[...]], axis=1)
    lb = both[PAD : PAD + cases]
    ld = both[PAD + cases : PAD + cases + 1]
    lifted_rhs[...] = lb
    lifted_scale[...] = ld
    m0 = tn(near[...], v)
    start[...] = m0[:, face:]
    image = times_schur(m0, high, low)
    image_out[...] = image
    to_even[...], to_odd[...] = split_sides(me[0], subs, image[:, face:], image[:, :face])
    shares = -nt(jnp.concatenate([v, v * ld], axis=0), image)
    mine = nt(jnp.concatenate([basis[...], basis[...] * ld], axis=0), lb)
    scaled = nt(basis[...] * ld, v)
    part = side_by_side(shares, 6)
    part[1] = part[1] + mine[:PAD]
    part[4] = part[4] + mine[PAD:]
    used = 6 * cases + 3 * PAD
    width = payload.shape[2]
    row = jnp.concatenate(part + [scaled, jnp.zeros((PAD, width - used), f32)], axis=1)
    payload[...] = jnp.broadcast_to(row[None], payload.shape)


def project_kernel(me, gathered, scaled, coarse, near, curvature, packed, padded, *, stride, k):
    nc, cases = packed.shape
    wide = gathered[...]
    g = gather_sum(wide, 0, cases, stride)
    h = gather_sum(wide, 3 * cases, cases, stride)
    c1 = coarse_times(coarse, nc, g, packed, k)
    c2 = coarse_times(
        coarse, nc, h - scaled_gram_times(scaled[...], 6 * cases, c1, k, stride // PAD), packed, k
    )
    near[: 3 * PAD] = near_blocks(c1, padded, me[0], stride)
    near[3 * PAD :] = near_blocks(c2, padded, me[0], stride)
    for b in range(cases // PAD):
        piece = wide[:, (6 + b) * cases : (7 + b) * cases]
        curvature[b * PAD : (b + 1) * PAD] = piece.reshape(-1, PAD, cases).sum(axis=0)


def direction_kernel(
    me, near, high, low, frame, lifted_rhs, lifted_scale, image_in, even_got, odd_got,
    search, residual, image_out, to_even, to_odd, payload, *, subs, chain,
):
    cases, face = even_got.shape
    from_left, from_right = join_sides(me[0], subs, chain, even_got[...], odd_got[...])
    moved = image_in[...] + jnp.concatenate([from_left, from_right], axis=1)
    v = frame[...]
    r = lifted_rhs[...] - moved - tn(near[: 3 * PAD], v)
    s = lifted_scale[...] * r - tn(near[3 * PAD :], v)
    search[...] = s
    residual[...] = r[:, face:]
    image = times_schur(s, high, low)
    image_out[...] = image
    to_even[...], to_odd[...] = split_sides(me[0], subs, image[:, face:], image[:, :face])
    shares = nt(jnp.concatenate([v, v * lifted_scale[...]], axis=0), image)
    energy = nt(s, image)
    part = side_by_side(shares, 6) + side_by_side(energy, cases // PAD)
    used = (6 + cases // PAD) * cases
    width = payload.shape[2]
    if width > used:
        part = part + [jnp.zeros((PAD, width - used), f32)]
    payload[...] = jnp.broadcast_to(jnp.concatenate(part, axis=1)[None], payload.shape)


def second_kernel(
    me, near, high, low, frame, lifted_scale, search, residual, image_in, even_got, odd_got,
    projected, second, image_out, to_even, to_odd, payload, *, subs, chain,
):
    cases, face = even_got.shape
    from_left, from_right = join_sides(me[0], subs, chain, even_got[...], odd_got[...])
    q = image_in[...] + jnp.concatenate([from_left, from_right], axis=1)
    v = frame[...]
    p = q - tn(near[: 3 * PAD], v)
    z = lifted_scale[...] * p - tn(near[3 * PAD :], v)
    projected[...] = p[:, face:]
    zr = z[:, face:]
    second[...] = zr
    image = times_schur(z, high, low)
    image_out[...] = image[:, face:]
    to_even[...], to_odd[...] = split_sides(me[0], subs, image[:, face:], image[:, :face])
    grams = nt(
        jnp.concatenate([search[:, face:], zr, q[:, face:]], axis=0),
        jnp.concatenate([residual[...], p[:, face:], zr], axis=0),
    )
    energy = nt(z, image)
    shares = side_by_side(nt(v, image), 3)
    top, bottom = grams[:cases, : 2 * cases], grams[cases : 2 * cases, : 2 * cases]
    crossed = grams[2 * cases :, 2 * cases :]
    extra_top = jnp.concatenate(shares[:2], axis=1)
    extra_low = jnp.concatenate([shares[2], jnp.zeros((PAD, cases), f32)], axis=1)
    extra = jnp.concatenate([extra_top, extra_low], axis=0)
    row = [top, crossed, bottom, energy, extra]
    used = 8 * cases
    width = payload.shape[2]
    if width > used:
        row = row + [jnp.zeros((cases, width - used), f32)]
    payload[...] = jnp.broadcast_to(jnp.concatenate(row, axis=1)[None], payload.shape)


def eliminate(matrix, right):
    n = matrix.shape[0]
    work = jnp.concatenate([matrix, right], axis=1)
    rows = lax.broadcasted_iota(jnp.int32, work.shape, 0)
    for i in range(n):
        row = work[i : i + 1] / work[i : i + 1, i : i + 1]
        work = jnp.where(rows == i, row, work - work[:, i : i + 1] * row)
    return work[:, n:]


def invert_kernel(curvature, inverse):
    n = curvature.shape[0]
    rows = lax.broadcasted_iota(jnp.int32, (n, n), 0)
    columns = lax.broadcasted_iota(jnp.int32, (n, n), 1)
    inverse[...] = eliminate(curvature[...], jnp.where(rows == columns, 1.0, 0.0))


def step_kernel(me, gathered, coarse, inverse, steps, packed, *, subs, chain, k):
    nc, cases = packed.shape
    all_of = gathered[...]
    peers = all_of.shape[0]
    total = all_of.sum(axis=0)
    sr, sp, qz, zr, zp, zw = [total[:, b * cases : (b + 1) * cases] for b in range(6)]
    low, mid = 6 * cases, 7 * cases
    part = [
        all_of[:, :PAD, low:mid],
        all_of[:, :PAD, mid : mid + cases],
        all_of[:, PAD : 2 * PAD, low:mid],
    ]
    none = jnp.zeros((subs, PAD, cases), f32)
    g = (
        part[1]
        + jnp.concatenate([part[0][subs:], none], axis=0)
        + jnp.concatenate([none, part[2][:-subs]], axis=0)
    ).reshape(peers * PAD, cases)
    for i in range(nc // k):
        packed[i * k : (i + 1) * k] = g[i * PAD : i * PAD + k]
    row = pl.multiple_of(me[0] * PAD, PAD)
    after = pl.multiple_of(jnp.minimum(me[0] + subs, peers - 1) * PAD, PAD)
    rows = jnp.concatenate([coarse[pl.ds(row, PAD), :nc], coarse[pl.ds(after, PAD), :nc]], axis=0)
    own = nn(rows, packed[...])
    solved = nn(inverse[...], jnp.concatenate([sr, qz], axis=1))
    a0, y = solved[:, :cases], solved[:, cases:]
    x = nn(y, a0)
    w1 = tn(a0, nn(zw, a0) - tn(qz, x))
    e1 = tn(x, sr - nn(sp, a0)) - tn(a0, zr - nn(zp, a0))
    a1 = eliminate(w1, e1)
    steps[:cases] = a0 + nn(x, a1)
    steps[cases : 2 * cases] = nn(a0, a1)
    steps[2 * cases :] = own


def finish_kernel(
    me, steps, frame, start, search, residual, projected, second, image, even_got, odd_got,
    out_mult, out_res, *, subs, chain,
):
    cases, face = start.shape
    _, from_right = join_sides(me[0], subs, chain, even_got[...], odd_got[...])
    w = image[...] + from_right - tn(steps[2 * cases :], frame[PAD : 3 * PAD, face:])
    first, last = steps[:cases], steps[cases : 2 * cases]
    out_mult[...] = start[...] + tn(first, search[:, face:]) - tn(last, second[...])
    out_res[...] = residual[...] - tn(first, projected[...]) + tn(last, w)


VMEM = pl.BlockSpec(memory_space=pltpu.VMEM)
SMEM = pl.BlockSpec(memory_space=pltpu.SMEM)
FAR = pl.BlockSpec(memory_space=pltpu.HBM)


def up(value, unit):
    return -(-value // unit) * unit


def call(kernel, args, outs, name, scratch=(), scalars=(0,), far=(), sems=0):
    shapes = [(a.shape, a.dtype) for i, a in enumerate(args) if i not in far + scalars]
    shapes = shapes + list(outs) + [(s, f32) for s in scratch if isinstance(s, tuple)]
    need = sum(math.prod(s[:-1]) * up(s[-1], 128) * jnp.dtype(d).itemsize for s, d in shapes)
    limit = 60 * 1024 * 1024 if far else min(2 * need + (6 << 20), 60 << 20)
    spaces = [SMEM if i in scalars else FAR if i in far else VMEM for i in range(len(args))]
    extra = [pltpu.SemaphoreType.DMA((sems,))] if sems else []
    return pl.pallas_call(
        kernel,
        out_shape=[jax.ShapeDtypeStruct(s, d) for s, d in outs],
        in_specs=spaces,
        out_specs=[VMEM] * len(outs),
        scratch_shapes=[s if not isinstance(s, tuple) else pltpu.VMEM(s, f32) for s in scratch] + extra,
        name=name,
        compiler_params=pltpu.CompilerParams(vmem_limit_bytes=limit),
    )(*args)


def exchange(to_even, to_odd):
    chain = lax.axis_size("cluster")
    subs = lax.axis_size("sub")
    even, odd = [], []
    for c in range(chain):
        for t in range(subs):
            even.append((c * subs + t, (c ^ 1) * subs + t))
            if c in (0, chain - 1):
                odd.append((c * subs + t, c * subs + (t ^ 1)))
            else:
                odd.append((c * subs + t, (((c + 1) ^ 1) - 1) * subs + t))
    return lax.ppermute(to_even, AXES, even), lax.ppermute(to_odd, AXES, odd)


def spread(payload):
    return lax.all_to_all(payload, AXES, 0, 0)


def shards(rhs, schur, modes, count, order, scale, load, coarse):
    chain = lax.axis_size("cluster")
    subs = lax.axis_size("sub")
    peers = chain * subs
    cases, face = rhs.shape[2:]
    size = schur.shape[2]
    k = modes.shape[2]
    nc = coarse.shape[1]
    stride = subs * PAD
    rows = peers * PAD
    me = (lax.axis_index("cluster") * subs + lax.axis_index("sub")).astype(jnp.int32).reshape(1)
    rhs, schur = rhs[0, 0], schur[0, 0]
    modes = modes[0].transpose(1, 0, 2)
    load = load[0].transpose(1, 0, 2)
    count = count.reshape(1)
    order = order.reshape(1, face)
    scale = scale.reshape(1, face)
    vec, lifted, small = (cases, face), (cases, size), (cases, cases)
    wide0 = up(nc + cases, 128)
    wide1 = up(6 * cases + 3 * PAD, 128)
    wide2 = up((6 + cases // PAD) * cases, 128)
    wide3 = up(8 * cases, 128)
    work = [(nc, cases), (rows + 2 * stride, cases)]
    packet = (up(PAD + cases + 1, 8), face)
    head = functools.partial
    line = {"subs": subs, "chain": chain}
    grid = {"stride": stride, "k": k}

    basis, own, to_even, to_odd, payload = call(
        head(pack_kernel, subs=subs),
        (me, count, modes, order, load, coarse, rhs, scale),
        [((PAD, size), f32), (packet, f32), (packet, f32), (packet, f32), ((peers, PAD, wide0), f32)],
        "pack",
        scratch=[modes.shape, pltpu.VMEM(order.shape, jnp.int32), load.shape, coarse.shape, vec, scale.shape],
        scalars=(0, 1),
        far=(2, 3, 4, 5, 6, 7),
        sems=6,
    )
    got = exchange(to_even, to_odd)
    coarse_rows = spread(payload).reshape(rows, wide0)
    high, low = call(
        head(permute_kernel, subs=subs),
        (me, order, schur),
        [((size, size), bf16), ((size, size), bf16)],
        "permute",
    )
    (near,) = call(
        head(load_kernel, **grid), (me, coarse_rows), [((3 * PAD, cases), f32)], "load", scratch=work
    )

    frame, lifted_rhs, lifted_scale, start, image, to_even, to_odd, payload = call(
        head(start_kernel, **line),
        (me, near, high, low, basis, own, *got),
        [
            ((3 * PAD, size), f32), (lifted, f32), ((1, size), f32), (vec, f32), (lifted, f32),
            (vec, f32), (vec, f32), ((peers, PAD, wide1), f32),
        ],
        "start",
    )
    got = exchange(to_even, to_odd)
    first = spread(payload).reshape(rows, wide1)
    near, _ = call(
        head(project_kernel, **grid),
        (me, first, first, coarse_rows),
        [((6 * PAD, cases), f32), (small, f32)],
        "project_start",
        scratch=work,
    )

    search, residual, image, to_even, to_odd, payload = call(
        head(direction_kernel, **line),
        (me, near, high, low, frame, lifted_rhs, lifted_scale, image, *got),
        [(lifted, f32), (vec, f32), (lifted, f32), (vec, f32), (vec, f32), ((peers, PAD, wide2), f32)],
        "direction",
    )
    got = exchange(to_even, to_odd)
    shared = spread(payload).reshape(rows, wide2)
    near, curvature = call(
        head(project_kernel, **grid),
        (me, shared, first, coarse_rows),
        [((6 * PAD, cases), f32), (small, f32)],
        "project_image",
        scratch=work,
    )

    projected, second, image, to_even, to_odd, payload = call(
        head(second_kernel, **line),
        (me, near, high, low, frame, lifted_scale, search, residual, image, *got),
        [(vec, f32), (vec, f32), (vec, f32), (vec, f32), (vec, f32), ((peers, cases, wide3), f32)],
        "second",
    )
    got = exchange(to_even, to_odd)
    shared = spread(payload)
    (inverse,) = call(invert_kernel, (curvature,), [(small, f32)], "invert", scalars=())
    (steps,) = call(
        head(step_kernel, k=k, **line),
        (me, shared, coarse_rows, inverse),
        [((2 * cases + 2 * PAD, cases), f32)],
        "step",
        scratch=[(nc, cases)],
    )
    multipliers, residual = call(
        head(finish_kernel, **line),
        (me, steps, frame, start, search, residual, projected, second, image, *got),
        [(vec, f32), (vec, f32)],
        "finish",
    )
    return multipliers[None, None], residual[None, None]


def solution(mesh):
    in_specs = (
        P("sub", "cluster", None, None),
        P("sub", "cluster", None, None),
        P("sub", "cluster", None, None),
        P("sub", "cluster"),
        P("sub", "cluster", None),
        P("sub", "cluster", None),
        P("sub", "cluster", None, None),
        P(("cluster", "sub"), None),
    )
    out_specs = (P("sub", "cluster", None, None), P("sub", "cluster", None, None))
    return jax.shard_map(shards, mesh=mesh, in_specs=in_specs, out_specs=out_specs, check_vma=False)
```

time: 97.5 us -> 70.3 us (0.72)
  starting transfers between devices: 44.7 us -> 22.2 us
  Pallas kernels: 26.6 us -> 18.8 us
  waiting for transfers between devices: 18 us -> 25.2 us
  local copies, waits for them, and re-layouts: 5.33 us -> 2.35 us
    all_to_all x4, waiting for transfers between devices: 8.49 us -> 25.2 us  [spread(): return lax.all_to_all(payload, AXES, 0, 0)]
    ppermute x7 -> x8, starting transfers between devices: 18.8 us -> 7.11 us  [exchange(): return (lax.ppermute(to_even, AXES, even), lax.ppermute(to_odd, AXES, odd))]
    all_to_all x4, starting transfers between devices: 25.9 us -> 15 us  [spread(): return lax.all_to_all(payload, AXES, 0, 0)]
    ppermute x7 -> x8, waiting for transfers between devices: 9.56 us -> 0.02 us  [exchange(): return (lax.ppermute(to_even, AXES, even), lax.ppermute(to_odd, AXES, odd))]
    pallas_call x5 -> x11, Pallas kernels: 26.6 us -> 18.8 us  [call(): pl.pallas_call(kernel, out_shape=[jax.ShapeDtypeStruct(s, d) for s, d in...]
    unnamed x24 -> x8, local copies, waits for them, and re-layouts: 5.33 us -> 2.35 us
  transfers between devices with their start and end apart: 11 -> 12, of which waited for: 10 -> 4; matrix products, arithmetic and copies ran while one was open for 1% -> 0% of each run, Pallas kernels for 0% -> 15%
where the time goes in v2:
time: 70.3 us; the launch traced here: 69.9 us
  waiting for transfers between devices  25.2 us (36%)
  starting transfers between devices  22.2 us (32%)
  Pallas kernels  18.8 us (27%)
  local copies, waits for them, and re-layouts  2.35 us (3%)
  between operations  1.41 us (2%)
    all_to_all x4, waiting for transfers between devices, spread(): return lax.all_to_all(payload, AXES, 0, 0)  25.2 us
    pallas_call x11, Pallas kernels, call(): pl.pallas_call(kernel, out_shape=[jax.ShapeDtypeStruct(s, d) for s, d in...  18.8 us
    all_to_all x4, starting transfers between devices, spread(): return lax.all_to_all(payload, AXES, 0, 0)  15 us
    ppermute x8, starting transfers between devices, exchange(): return (lax.ppermute(to_even, AXES, even), lax.ppermute(to_odd, AXES, odd))  7.11 us
    unnamed x8, local copies, waits for them, and re-layouts  2.35 us
  transfers between devices with their start and end apart: 12, of which 4 were waited for; matrix products, arithmetic and copies ran while one was open for 0% of the time, Pallas kernels for 15%

profile of v2, /device:TPU:0, one launch (start us, length us, event | category | flops | bytes accessed | tf_op | source)
XLA Modules:
  0.0 69.9 jit_solution(14175892590011886681)
XLA Ops:
  1.3 2.0 %pack.1 = (f32[8,768]{1,0:T(8,128)}, f32[32,384]{1,0:T(8,128)}, f32[32,384]{1,0:T(8,128)}, f32[32,384]{1,0:T(8,128)}, f32[32,8,256]{2,1,0:T(8,128)}) custom-call(s32[1]{0:T(128)} %bitcast.me, s32[1]{0:T(128)} %bitcast.13.count, f32[6,1,768]{2,1,0:T(1,128)} %bitcast.26, s32[1,384]{1,0:T(1,128)} %bitcast.23, f32[6,1,16]{2,1,0:T(1,128)} %bitcast.27, ...), custom_call_target="tpu_custom_call" | custom-call | tf_op jit(solution)/shard_map/pack/pallas_call | solution.py:382
  3.3 7.3 %all-to-all-start = ((f32[32,8,256]{2,1,0:T(8,128)}), f32[32,8,256]{2,1,0:T(8,128)S(1)}, u32[]{:S(2)}, u32[]{:S(2)}) async-start(f32[32,8,256]{2,1,0:T(8,128)} %get-tuple-element.34), calls=%async_computation | async-start | bytes 524288 | tf_op jit(solution)/shard_map/all_to_all | solution.py:408
  10.6 1.8 %collective-permute-start = (f32[32,384]{1,0:T(8,128)}, f32[32,384]{1,0:T(8,128)S(1)}, u32[]{:S(2)}, u32[]{:S(2)}) collective-permute-start(f32[32,384]{1,0:T(8,128)} %get-tuple-element.39), channel_id=1, source_target_pairs={{0,4},{1,5},{2,6},{3,7},{4,0},{5,1},{6,2},{7,3},{8,12},{9,13},{10,... | collective-permute-start | bytes 147464 | tf_op jit(solution)/shard_map/ppermute | solution.py:404
  12.4 1.7 %copy-done = f32[1,1,768,768]{3,2,1,0:T(8,128)S(1)} copy-done((f32[1,1,768,768]{3,2,1,0:T(8,128)S(1)}, f32[1,1,768,768]{3,2,1,0:T(8,128)}, u32[]{:S(2)}) %copy-start) | copy-done | bytes 2359320
  14.1 0.7 copy-done.3
  14.8 1.6 %permute.1 = (bf16[768,768]{1,0:T(8,128)(2,1)S(1)}, bf16[768,768]{1,0:T(8,128)(2,1)S(1)}) custom-call(s32[1]{0:T(128)} %bitcast.me, s32[1,384]{1,0:T(1,128)S(1)} %bitcast.24, f32[768,768]{1,0:T(8,128)S(1)} %bitcast.18), custom_call_target="tpu_custom_call" | custom-call | tf_op jit(solution)/shard_map/permute/pallas_call | solution.py:382
  16.4 4.8 %all-to-all-done = f32[32,8,256]{2,1,0:T(8,128)S(1)} async-done(((f32[32,8,256]{2,1,0:T(8,128)}), f32[32,8,256]{2,1,0:T(8,128)S(1)}, u32[]{:S(2)}, u32[]{:S(2)}) %all-to-all-start) | async-done | bytes 262176 | tf_op jit(solution)/shard_map/all_to_all | solution.py:408
  21.2 0.5 load.1.near
  21.6 0.0 collective-permute-done.1.odd_got
  21.7 1.9 %start.1 = (f32[24,768]{1,0:T(8,128)S(1)}, f32[16,768]{1,0:T(8,128)S(1)}, f32[1,768]{1,0:T(1,128)S(1)}, f32[16,384]{1,0:T(8,128)S(1)}, f32[16,768]{1,0:T(8,128)S...) custom-call(s32[1]{0:T(128)} %bitcast.me, f32[24,16]{1,0:T(8,128)S(1)} %load.1.near, ...), custom_call_target="tpu_custom_call" | custom-call | tf_op jit(solution)/shard_map/start/pallas_call | solution.py:382
  23.6 2.6 %all-to-all-start.1 = ((f32[32,8,128]{2,1,0:T(8,128)}), f32[32,8,128]{2,1,0:T(8,128)S(1)}, u32[]{:S(2)}, u32[]{:S(2)}) async-start(f32[32,8,128]{2,1,0:T(8,128)} %get-tuple-element.41), calls=%async_computation.1 | async-start | bytes 262144 | tf_op jit(solution)/shard_map/all_to_all | solution.py:408
  26.1 1.8 %collective-permute-start.2 = (f32[16,384]{1,0:T(8,128)S(1)}, f32[16,384]{1,0:T(8,128)S(1)}, u32[]{:S(2)}, u32[]{:S(2)}) collective-permute-start(f32[16,384]{1,0:T(8,128)S(1)} %get-tuple-element.47), channel_id=1, source_target_pairs={{0,4},{1,5},{2,6},{3,7},{4,0},{5,1},{6,2},{7,3},{8,12},{9,13},{10,... | collective-permute-start | bytes 73736 | tf_op jit(solution)/shard_map/ppermute | solution.py:404
  28.0 6.4 %all-to-all-done.1 = f32[32,8,128]{2,1,0:T(8,128)S(1)} async-done(((f32[32,8,128]{2,1,0:T(8,128)}), f32[32,8,128]{2,1,0:T(8,128)S(1)}, u32[]{:S(2)}, u32[]{:S(2)}) %all-to-all-start.1) | async-done | bytes 131104 | tf_op jit(solution)/shard_map/all_to_all | solution.py:408
  34.3 2.4 %project_start.1 = (f32[48,16]{1,0:T(8,128)S(1)}, f32[16,16]{1,0:T(8,128)}) custom-call(s32[1]{0:T(128)} %bitcast.me, f32[256,128]{1,0:T(8,128)S(1)} %bitcast.19, f32[256,128]{1,0:T(8,128)S(1)} %bitcast.20, f32[256,256]{1,0:T(8,128)S(1)} %bitcast.15), custom_call_target="tpu_custom_call" | custom-call | tf_op jit(solution)/shard_map/project_start/pallas_call | solution.py:382
  36.7 0.0 collective-permute-done.2.even_got
  36.7 0.0 collective-permute-done.3.odd_got
  36.7 1.8 %direction.1 = (f32[16,768]{1,0:T(8,128)S(1)}, f32[16,384]{1,0:T(8,128)S(1)}, f32[16,768]{1,0:T(8,128)S(1)}, f32[16,384]{1,0:T(8,128)S(1)}, f32[16,384]{1,0:T(8,128)S(1)}, /*index=5*/f32[32,8,128]{2,1,0:T(8,128)}) custom-call(s32[1]{0:T(128)} %bitcast.me, f32[48,16]{1,0:T(8,128)S(1)} %get-tuple-element.42.near, bf16[768,768]{1,0:T(8,128)(2,1)S(1)} %get-tuple-element.35.high, ...), custom_call_target="tpu_custom_call" | custom-call | tf_op jit(solution)/shard_map/direction/pallas_call | solution.py:382
  38.5 2.6 %all-to-all-start.2 = ((f32[32,8,128]{2,1,0:T(8,128)}), f32[32,8,128]{2,1,0:T(8,128)S(1)}, u32[]{:S(2)}, u32[]{:S(2)}) async-start(f32[32,8,128]{2,1,0:T(8,128)} %get-tuple-element.49), calls=%async_computation.2 | async-start | bytes 262144 | tf_op jit(solution)/shard_map/all_to_all | solution.py:408
  41.1 1.7 %collective-permute-start.4 = (f32[16,384]{1,0:T(8,128)S(1)}, f32[16,384]{1,0:T(8,128)S(1)}, u32[]{:S(2)}, u32[]{:S(2)}) collective-permute-start(f32[16,384]{1,0:T(8,128)S(1)} %get-tuple-element.54), channel_id=1, source_target_pairs={{0,4},{1,5},{2,6},{3,7},{4,0},{5,1},{6,2},{7,3},{8,12},{9,13},{10,... | collective-permute-start | bytes 73736 | tf_op jit(solution)/shard_map/ppermute | solution.py:404
  42.8 0.0 collective-permute-start.5
  42.8 6.5 %all-to-all-done.2 = f32[32,8,128]{2,1,0:T(8,128)S(1)} async-done(((f32[32,8,128]{2,1,0:T(8,128)}), f32[32,8,128]{2,1,0:T(8,128)S(1)}, u32[]{:S(2)}, u32[]{:S(2)}) %all-to-all-start.2) | async-done | bytes 131104 | tf_op jit(solution)/shard_map/all_to_all | solution.py:408
  49.3 1.8 %project_image.1 = (f32[48,16]{1,0:T(8,128)S(1)}, f32[16,16]{1,0:T(8,128)S(1)}) custom-call(s32[1]{0:T(128)} %bitcast.me, f32[256,128]{1,0:T(8,128)S(1)} %bitcast.22, f32[256,128]{1,0:T(8,128)S(1)} %bitcast.21, f32[256,256]{1,0:T(8,128)S(1)} %bitcast.16), custom_call_target="tpu_custom_call" | custom-call | tf_op jit(solution)/shard_map/project_image/pallas_call | solution.py:382
  51.1 0.0 collective-permute-done.5.odd_got
  51.1 1.8 %second.1 = (f32[16,384]{1,0:T(8,128)S(1)}, f32[16,384]{1,0:T(8,128)S(1)}, f32[16,384]{1,0:T(8,128)S(1)}, f32[16,384]{1,0:T(8,128)S(1)}, f32[16,384]{1,0:T(8,128)S(1)}, /*index=5*/f32[32,16,128]{2,1,0:T(8,128)}) custom-call(s32[1]{0:T(128)} %bitcast.me, f32[48,16]{1,0:T(8,128)S(1)} %get-tuple-element.50.near, bf16[768,768]{1,0:T(8,128)(2,1)S(1)} %get-tuple-element.35.high, ...), custom_call_target="tpu_custom_call" | custom-call | tf_op jit(solution)/shard_map/second/pallas_call | solution.py:382
  52.9 2.6 %all-to-all-start.3 = ((f32[32,16,128]{2,1,0:T(8,128)}), f32[32,16,128]{2,1,0:T(8,128)S(1)}, u32[]{:S(2)}, u32[]{:S(2)}) async-start(f32[32,16,128]{2,1,0:T(8,128)} %get-tuple-element.56), calls=%async_computation.3 | async-start | bytes 524288 | tf_op jit(solution)/shard_map/all_to_all | solution.py:408
  55.5 1.7 %collective-permute-start.6 = (f32[16,384]{1,0:T(8,128)S(1)}, f32[16,384]{1,0:T(8,128)S(1)}, u32[]{:S(2)}, u32[]{:S(2)}) collective-permute-start(f32[16,384]{1,0:T(8,128)S(1)} %get-tuple-element.62), channel_id=1, source_target_pairs={{0,4},{1,5},{2,6},{3,7},{4,0},{5,1},{6,2},{7,3},{8,12},{9,13},{10,... | collective-permute-start | bytes 73736 | tf_op jit(solution)/shard_map/ppermute | solution.py:404
  57.2 0.0 collective-permute-start.7
  57.2 1.3 %invert.1.inverse = f32[16,16]{1,0:T(8,128)S(1)} custom-call(f32[16,16]{1,0:T(8,128)S(1)} %get-tuple-element.57.curvature), custom_call_target="tpu_custom_call" | custom-call | tf_op jit(solution)/shard_map/invert/pallas_call | solution.py:382
  58.5 7.5 %all-to-all-done.3.gathered = f32[32,16,128]{2,1,0:T(8,128)S(1)} async-done(((f32[32,16,128]{2,1,0:T(8,128)}), f32[32,16,128]{2,1,0:T(8,128)S(1)}, u32[]{:S(2)}, u32[]{:S(2)}) %all-to-all-start.3) | async-done | bytes 262176 | tf_op jit(solution)/shard_map/all_to_all | solution.py:408
  66.1 2.7 %step.1.steps = f32[48,16]{1,0:T(8,128)S(1)} custom-call(s32[1]{0:T(128)} %bitcast.me, f32[32,16,128]{2,1,0:T(8,128)S(1)} %all-to-all-done.3.gathered, f32[256,256]{1,0:T(8,128)S(1)} %bitcast.17, f32[16,16]{1,0:T(8,128)S(1)} %invert.1.inverse), custom_call_target="tpu_custom_call" | custom-call | tf_op jit(solution)/shard_map/step/pallas_call | solution.py:382
  68.8 0.0 collective-permute-done.6.even_got
  68.8 1.0 %finish.1 = (f32[16,384]{1,0:T(8,128)}, f32[16,384]{1,0:T(8,128)}) custom-call(s32[1]{0:T(128)} %bitcast.me, f32[48,16]{1,0:T(8,128)S(1)} %step.1.steps, f32[24,768]{1,0:T(8,128)S(1)} %get-tuple-element.43.frame, f32[16,384]{1,0:T(8,128)S(1)} %get-tuple-element.58.start, f32[16,768]{1,0:T(8,128)S(1)} %get-tuple-element.51.search, ...), custom_call_target="tpu_custom_call" | custom-call | tf_op jit(solution)/shard_map/finish/pallas_call | solution.py:382
  (11 shorter events, 0.0 us)
Async XLA Ops:
  3.3 17.9 %all-to-all-start = ((f32[32,8,256]{2,1,0:T(8,128)}), f32[32,8,256]{2,1,0:T(8,128)S(1)}, u32[]{:S(2)}, u32[]{:S(2)}) async-start(f32[32,8,256]{2,1,0:T(8,128)} %get-tuple-element.34), calls=%async_computation | async-start | bytes 524288 | tf_op jit(solution)/shard_map/all_to_all | solution.py:408
  10.6 11.0 %collective-permute-start = (f32[32,384]{1,0:T(8,128)}, f32[32,384]{1,0:T(8,128)S(1)}, u32[]{:S(2)}, u32[]{:S(2)}) collective-permute-start(f32[32,384]{1,0:T(8,128)} %get-tuple-element.39), channel_id=1, source_target_pairs={{0,4},{1,5},{2,6},{3,7},{4,0},{5,1},{6,2},{7,3},{8,12},{9,13},{10,... | collective-permute-start | bytes 147464 | tf_op jit(solution)/shard_map/ppermute | solution.py:404
  12.4 9.2 %collective-permute-start.1 = (f32[32,384]{1,0:T(8,128)}, f32[32,384]{1,0:T(8,128)S(1)}, u32[]{:S(2)}, u32[]{:S(2)}) collective-permute-start(f32[32,384]{1,0:T(8,128)} %get-tuple-element.40), channel_id=1, source_target_pairs={{0,1},{1,0},{2,3},{3,2},{4,8},{5,9},{6,10},{7,11},{8,4},{9,5},{10,... | collective-permute-start | bytes 147464 | tf_op jit(solution)/shard_map/ppermute | solution.py:404
  12.4 1.7 %copy-start = (f32[1,1,768,768]{3,2,1,0:T(8,128)S(1)}, f32[1,1,768,768]{3,2,1,0:T(8,128)}, u32[]{:S(2)}) copy-start(f32[1,1,768,768]{3,2,1,0:T(8,128)} %param.9) | copy-start | bytes 7077892
  14.1 0.7 copy-start.3
  14.8 6.9 %copy-start.1 = (f32[32,384]{1,0:T(8,128)S(1)}, f32[32,384]{1,0:T(8,128)}, u32[]{:S(2)}) copy-start(f32[32,384]{1,0:T(8,128)} %get-tuple-element.38.own) | copy-start | bytes 147460
  14.8 6.9 %copy-start.2 = (f32[8,768]{1,0:T(8,128)S(1)}, f32[8,768]{1,0:T(8,128)}, u32[]{:S(2)}) copy-start(f32[8,768]{1,0:T(8,128)} %get-tuple-element.37.basis) | copy-start | bytes 73732
  23.6 10.8 %all-to-all-start.1 = ((f32[32,8,128]{2,1,0:T(8,128)}), f32[32,8,128]{2,1,0:T(8,128)S(1)}, u32[]{:S(2)}, u32[]{:S(2)}) async-start(f32[32,8,128]{2,1,0:T(8,128)} %get-tuple-element.41), calls=%async_computation.1 | async-start | bytes 262144 | tf_op jit(solution)/shard_map/all_to_all | solution.py:408
  26.1 10.6 %collective-permute-start.2 = (f32[16,384]{1,0:T(8,128)S(1)}, f32[16,384]{1,0:T(8,128)S(1)}, u32[]{:S(2)}, u32[]{:S(2)}) collective-permute-start(f32[16,384]{1,0:T(8,128)S(1)} %get-tuple-element.47), channel_id=1, source_target_pairs={{0,4},{1,5},{2,6},{3,7},{4,0},{5,1},{6,2},{7,3},{8,12},{9,13},{10,... | collective-permute-start | bytes 73736 | tf_op jit(solution)/shard_map/ppermute | solution.py:404
  28.0 8.7 %collective-permute-start.3 = (f32[16,384]{1,0:T(8,128)S(1)}, f32[16,384]{1,0:T(8,128)S(1)}, u32[]{:S(2)}, u32[]{:S(2)}) collective-permute-start(f32[16,384]{1,0:T(8,128)S(1)} %get-tuple-element.48), channel_id=1, source_target_pairs={{0,1},{1,0},{2,3},{3,2},{4,8},{5,9},{6,10},{7,11},{8,4},{9,5},{10,... | collective-permute-start | bytes 73736 | tf_op jit(solution)/shard_map/ppermute | solution.py:404
  38.5 10.8 %all-to-all-start.2 = ((f32[32,8,128]{2,1,0:T(8,128)}), f32[32,8,128]{2,1,0:T(8,128)S(1)}, u32[]{:S(2)}, u32[]{:S(2)}) async-start(f32[32,8,128]{2,1,0:T(8,128)} %get-tuple-element.49), calls=%async_computation.2 | async-start | bytes 262144 | tf_op jit(solution)/shard_map/all_to_all | solution.py:408
  41.1 10.0 %collective-permute-start.4 = (f32[16,384]{1,0:T(8,128)S(1)}, f32[16,384]{1,0:T(8,128)S(1)}, u32[]{:S(2)}, u32[]{:S(2)}) collective-permute-start(f32[16,384]{1,0:T(8,128)S(1)} %get-tuple-element.54), channel_id=1, source_target_pairs={{0,4},{1,5},{2,6},{3,7},{4,0},{5,1},{6,2},{7,3},{8,12},{9,13},{10,... | collective-permute-start | bytes 73736 | tf_op jit(solution)/shard_map/ppermute | solution.py:404
  42.8 8.3 %collective-permute-start.5 = (f32[16,384]{1,0:T(8,128)S(1)}, f32[16,384]{1,0:T(8,128)S(1)}, u32[]{:S(2)}, u32[]{:S(2)}) collective-permute-start(f32[16,384]{1,0:T(8,128)S(1)} %get-tuple-element.55), channel_id=1, source_target_pairs={{0,1},{1,0},{2,3},{3,2},{4,8},{5,9},{6,10},{7,11},{8,4},{9,5},{10,... | collective-permute-start | bytes 73736 | tf_op jit(solution)/shard_map/ppermute | solution.py:404
  52.9 13.2 %all-to-all-start.3 = ((f32[32,16,128]{2,1,0:T(8,128)}), f32[32,16,128]{2,1,0:T(8,128)S(1)}, u32[]{:S(2)}, u32[]{:S(2)}) async-start(f32[32,16,128]{2,1,0:T(8,128)} %get-tuple-element.56), calls=%async_computation.3 | async-start | bytes 524288 | tf_op jit(solution)/shard_map/all_to_all | solution.py:408
  55.5 13.3 %collective-permute-start.6 = (f32[16,384]{1,0:T(8,128)S(1)}, f32[16,384]{1,0:T(8,128)S(1)}, u32[]{:S(2)}, u32[]{:S(2)}) collective-permute-start(f32[16,384]{1,0:T(8,128)S(1)} %get-tuple-element.62), channel_id=1, source_target_pairs={{0,4},{1,5},{2,6},{3,7},{4,0},{5,1},{6,2},{7,3},{8,12},{9,13},{10,... | collective-permute-start | bytes 73736 | tf_op jit(solution)/shard_map/ppermute | solution.py:404
  57.2 11.6 %collective-permute-start.7 = (f32[16,384]{1,0:T(8,128)S(1)}, f32[16,384]{1,0:T(8,128)S(1)}, u32[]{:S(2)}, u32[]{:S(2)}) collective-permute-start(f32[16,384]{1,0:T(8,128)S(1)} %get-tuple-element.63), channel_id=1, source_target_pairs={{0,1},{1,0},{2,3},{3,2},{4,8},{5,9},{6,10},{7,11},{8,4},{9,5},{10,... | collective-permute-start | bytes 73736 | tf_op jit(solution)/shard_map/ppermute | solution.py:404

commit v3 on v2

--- a/solution.py
+++ b/solution.py
@@ -87,7 +87,6 @@
     copies = [pltpu.make_async_copy(a, b, sems.at[i]) for i, (a, b) in enumerate(pairs)]
     for copy in copies:
         copy.start()
-    payload[...] = jnp.zeros_like(payload)
     own[...] = jnp.zeros_like(own)
     basis[...] = jnp.zeros_like(basis)
     face = order.shape[1]
@@ -111,10 +110,12 @@
         me[0], subs, own[...], jnp.concatenate([left, rest], axis=0)
     )
     peers = payload.shape[0]
-    payload[:, :k, :nc] = jnp.broadcast_to(coarse[...][None], (peers, k, nc))
+    each = nc + cases
+    line = []
     for i in range(k):
-        row = jnp.where(i < count[0], load[i], 0.0)
-        payload[:, i : i + 1, nc : nc + cases] = jnp.broadcast_to(row[None], (peers, 1, cases))
+        line = line + [coarse[i : i + 1], jnp.where(i < count[0], load[i], 0.0)]
+    line = line + [jnp.zeros((1, payload.shape[2] - k * each), f32)]
+    payload[...] = jnp.broadcast_to(jnp.concatenate(line, axis=1)[None], payload.shape)
 
 
 def permute_kernel(me, order, schur, high, low, *, subs):
@@ -178,10 +179,17 @@
     return [tall[b * PAD : (b + 1) * PAD] for b in range(blocks)]
 
 
-def load_kernel(me, gathered, near, packed, padded, *, stride, k):
+def load_kernel(me, gathered, near, rows, packed, padded, *, stride, k):
     nc, cases = packed.shape
-    y = coarse_times(gathered, nc, gathered[:, nc : nc + cases], packed, k)
-    near[...] = near_blocks(y, padded, me[0], stride)
+    each = nc + cases
+    peers = gathered.shape[0]
+    rows[...] = jnp.zeros_like(rows)
+    for i in range(k):
+        rows[:, i, :each] = gathered[:, 0, i * each : (i + 1) * each]
+    for i in range(peers):
+        packed[i * k : (i + 1) * k] = rows[i, :k, nc:each]
+    table = rows[:, :, :nc].reshape(peers * PAD, nc)
+    near[...] = near_blocks(nn(table, packed[...]), padded, me[0], stride)
 
 
 def start_kernel(
@@ -223,7 +231,7 @@
     payload[...] = jnp.broadcast_to(row[None], payload.shape)
 
 
-def project_kernel(me, gathered, scaled, coarse, near, curvature, packed, padded, *, stride, k):
+def project_kernel(me, gathered, scaled, coarse, near, curvature, packed, padded, *, stride, k, total):
     nc, cases = packed.shape
     wide = gathered[...]
     g = gather_sum(wide, 0, cases, stride)
@@ -234,7 +242,9 @@
     )
     near[: 3 * PAD] = near_blocks(c1, padded, me[0], stride)
     near[3 * PAD :] = near_blocks(c2, padded, me[0], stride)
-    for b in range(cases // PAD):
+    if not total:
+        curvature[...] = jnp.zeros_like(curvature)
+    for b in range(cases // PAD if total else 0):
         piece = wide[:, (6 + b) * cases : (7 + b) * cases]
         curvature[b * PAD : (b + 1) * PAD] = piece.reshape(-1, PAD, cases).sum(axis=0)
 
@@ -427,6 +437,7 @@
     scale = scale.reshape(1, face)
     vec, lifted, small = (cases, face), (cases, size), (cases, cases)
     wide0 = up(nc + cases, 128)
+    flat0 = up(k * (nc + cases), 128)
     wide1 = up(6 * cases + 3 * PAD, 128)
     wide2 = up((6 + cases // PAD) * cases, 128)
     wide3 = up(8 * cases, 128)
@@ -439,7 +450,7 @@
     basis, own, to_even, to_odd, payload = call(
         head(pack_kernel, subs=subs),
         (me, count, modes, order, load, coarse, rhs, scale),
-        [((PAD, size), f32), (packet, f32), (packet, f32), (packet, f32), ((peers, PAD, wide0), f32)],
+        [((PAD, size), f32), (packet, f32), (packet, f32), (packet, f32), ((peers, 1, flat0), f32)],
         "pack",
         scratch=[modes.shape, pltpu.VMEM(order.shape, jnp.int32), load.shape, coarse.shape, vec, scale.shape],
         scalars=(0, 1),
@@ -447,16 +458,21 @@
         sems=6,
     )
     got = exchange(to_even, to_odd)
-    coarse_rows = spread(payload).reshape(rows, wide0)
+    shared = spread(payload)
     high, low = call(
         head(permute_kernel, subs=subs),
         (me, order, schur),
         [((size, size), bf16), ((size, size), bf16)],
         "permute",
     )
-    (near,) = call(
-        head(load_kernel, **grid), (me, coarse_rows), [((3 * PAD, cases), f32)], "load", scratch=work
-    )
+    near, coarse_rows = call(
+        head(load_kernel, **grid),
+        (me, shared),
+        [((3 * PAD, cases), f32), ((peers, PAD, wide0), f32)],
+        "load",
+        scratch=work,
+    )
+    coarse_rows = coarse_rows.reshape(rows, wide0)
 
     frame, lifted_rhs, lifted_scale, start, image, to_even, to_odd, payload = call(
         head(start_kernel, **line),
@@ -470,7 +486,7 @@
     got = exchange(to_even, to_odd)
     first = spread(payload).reshape(rows, wide1)
     near, _ = call(
-        head(project_kernel, **grid),
+        head(project_kernel, total=False, **grid),
         (me, first, first, coarse_rows),
         [((6 * PAD, cases), f32), (small, f32)],
         "project_start",
@@ -486,7 +502,7 @@
     got = exchange(to_even, to_odd)
     shared = spread(payload).reshape(rows, wide2)
     near, curvature = call(
-        head(project_kernel, **grid),
+        head(project_kernel, total=True, **grid),
         (me, shared, first, coarse_rows),
         [((6 * PAD, cases), f32), (small, f32)],
         "project_image",

time: 70.3 us -> 68.9 us (0.980)
  waiting for transfers between devices: 25.2 us -> 23.2 us
    all_to_all x4, waiting for transfers between devices: 25.2 us -> 23.2 us  [spread(): return lax.all_to_all(payload, AXES, 0, 0)]
    all_to_all x4, starting transfers between devices: 15 us -> 15.8 us  [spread(): return lax.all_to_all(payload, AXES, 0, 0)]
where the time goes in v3:
time: 68.9 us; the launch traced here: 68.5 us
  waiting for transfers between devices  23.2 us (34%)
  starting transfers between devices  22.9 us (33%)
  Pallas kernels  18.6 us (27%)
  local copies, waits for them, and re-layouts  2.35 us (3%)
  between operations  1.41 us (2%)
    all_to_all x4, waiting for transfers between devices, spread(): return lax.all_to_all(payload, AXES, 0, 0)  23.2 us
    pallas_call x11, Pallas kernels, call(): pl.pallas_call(kernel, out_shape=[jax.ShapeDtypeStruct(s, d) for s, d in...  18.6 us
    all_to_all x4, starting transfers between devices, spread(): return lax.all_to_all(payload, AXES, 0, 0)  15.8 us
    ppermute x8, starting transfers between devices, exchange(): return (lax.ppermute(to_even, AXES, even), lax.ppermute(to_odd, AXES, odd))  7.11 us
    unnamed x8, local copies, waits for them, and re-layouts  2.35 us
  transfers between devices with their start and end apart: 12, of which 4 were waited for; matrix products, arithmetic and copies ran while one was open for 0% of the time, Pallas kernels for 15%

profile of v3, /device:TPU:0, one launch (start us, length us, event | category | flops | bytes accessed | tf_op | source)
XLA Modules:
  0.0 68.5 jit_solution(11450872903928202855)
XLA Ops:
  1.3 1.9 %pack.1 = (f32[8,768]{1,0:T(8,128)}, f32[32,384]{1,0:T(8,128)}, f32[32,384]{1,0:T(8,128)}, f32[32,384]{1,0:T(8,128)}, f32[32,1,1280]{2,1,0:T(1,128)}) custom-call(s32[1]{0:T(128)} %bitcast.me, s32[1]{0:T(128)} %bitcast.13.count, f32[6,1,768]{2,1,0:T(1,128)} %bitcast.25, s32[1,384]{1,0:T(1,128)} %bitcast.22, f32[6,1,16]{2,1,0:T(1,128)} %bitcast.26, ...), custom_call_target="tpu_custom_call" | custom-call | tf_op jit(solution)/shard_map/pack/pallas_call | solution.py:392
  3.2 7.3 %all-to-all-start = ((f32[32,1,1280]{2,1,0:T(1,128)}), f32[32,1,1280]{2,1,0:T(1,128)S(1)}, u32[]{:S(2)}, u32[]{:S(2)}) async-start(f32[32,1,1280]{2,1,0:T(1,128)} %get-tuple-element.36), calls=%async_computation | async-start | bytes 327680 | tf_op jit(solution)/shard_map/all_to_all | solution.py:418
  10.6 1.8 %collective-permute-start = (f32[32,384]{1,0:T(8,128)}, f32[32,384]{1,0:T(8,128)S(1)}, u32[]{:S(2)}, u32[]{:S(2)}) collective-permute-start(f32[32,384]{1,0:T(8,128)} %get-tuple-element.42), channel_id=1, source_target_pairs={{0,4},{1,5},{2,6},{3,7},{4,0},{5,1},{6,2},{7,3},{8,12},{9,13},{10,... | collective-permute-start | bytes 147464 | tf_op jit(solution)/shard_map/ppermute | solution.py:414
  12.4 0.0 collective-permute-start.1
  12.4 1.7 %copy-done = f32[1,1,768,768]{3,2,1,0:T(8,128)S(1)} copy-done((f32[1,1,768,768]{3,2,1,0:T(8,128)S(1)}, f32[1,1,768,768]{3,2,1,0:T(8,128)}, u32[]{:S(2)}) %copy-start) | copy-done | bytes 2359320
  14.1 0.7 copy-done.3
  14.8 1.6 %permute.1 = (bf16[768,768]{1,0:T(8,128)(2,1)S(1)}, bf16[768,768]{1,0:T(8,128)(2,1)S(1)}) custom-call(s32[1]{0:T(128)} %bitcast.me, s32[1,384]{1,0:T(1,128)S(1)} %bitcast.23, f32[768,768]{1,0:T(8,128)S(1)} %bitcast.17), custom_call_target="tpu_custom_call" | custom-call | tf_op jit(solution)/shard_map/permute/pallas_call | solution.py:392
  16.4 2.8 %all-to-all-done.gathered = f32[32,1,1280]{2,1,0:T(1,128)S(1)} async-done(((f32[32,1,1280]{2,1,0:T(1,128)}), f32[32,1,1280]{2,1,0:T(1,128)S(1)}, u32[]{:S(2)}, u32[]{:S(2)}) %all-to-all-start) | async-done | bytes 163872 | tf_op jit(solution)/shard_map/all_to_all | solution.py:418
  19.2 0.7 load.1
  19.9 1.9 %start.1 = (f32[24,768]{1,0:T(8,128)S(1)}, f32[16,768]{1,0:T(8,128)S(1)}, f32[1,768]{1,0:T(1,128)S(1)}, f32[16,384]{1,0:T(8,128)S(1)}, f32[16,768]{1,0:T(8,128)S...) custom-call(s32[1]{0:T(128)} %bitcast.me, f32[24,16]{1,0:T(8,128)S(1)} %get-tuple-element.37.near, ...), custom_call_target="tpu_custom_call" | custom-call | tf_op jit(solution)/shard_map/start/pallas_call | solution.py:392
  21.8 3.3 %all-to-all-start.1 = ((f32[32,8,128]{2,1,0:T(8,128)}), f32[32,8,128]{2,1,0:T(8,128)S(1)}, u32[]{:S(2)}, u32[]{:S(2)}) async-start(f32[32,8,128]{2,1,0:T(8,128)} %get-tuple-element.44), calls=%async_computation.1 | async-start | bytes 262144 | tf_op jit(solution)/shard_map/all_to_all | solution.py:418
  25.1 1.8 %collective-permute-start.2 = (f32[16,384]{1,0:T(8,128)S(1)}, f32[16,384]{1,0:T(8,128)S(1)}, u32[]{:S(2)}, u32[]{:S(2)}) collective-permute-start(f32[16,384]{1,0:T(8,128)S(1)} %get-tuple-element.51), channel_id=1, source_target_pairs={{0,4},{1,5},{2,6},{3,7},{4,0},{5,1},{6,2},{7,3},{8,12},{9,13},{10,... | collective-permute-start | bytes 73736 | tf_op jit(solution)/shard_map/ppermute | solution.py:414
  26.9 0.0 collective-permute-start.3
  26.9 6.4 %all-to-all-done.1 = f32[32,8,128]{2,1,0:T(8,128)S(1)} async-done(((f32[32,8,128]{2,1,0:T(8,128)}), f32[32,8,128]{2,1,0:T(8,128)S(1)}, u32[]{:S(2)}, u32[]{:S(2)}) %all-to-all-start.1) | async-done | bytes 131104 | tf_op jit(solution)/shard_map/all_to_all | solution.py:418
  33.3 1.9 %project_start.1 = (f32[48,16]{1,0:T(8,128)S(1)}, f32[16,16]{1,0:T(8,128)}) custom-call(s32[1]{0:T(128)} %bitcast.me, f32[256,128]{1,0:T(8,128)S(1)} %bitcast.18, f32[256,128]{1,0:T(8,128)S(1)} %bitcast.19, f32[256,256]{1,0:T(8,128)S(1)} %bitcast.14), custom_call_target="tpu_custom_call" | custom-call | tf_op jit(solution)/shard_map/project_start/pallas_call | solution.py:392
  35.2 0.0 collective-permute-done.2.even_got
  35.3 0.0 collective-permute-done.3.odd_got
  35.3 1.8 %direction.1 = (f32[16,768]{1,0:T(8,128)S(1)}, f32[16,384]{1,0:T(8,128)S(1)}, f32[16,768]{1,0:T(8,128)S(1)}, f32[16,384]{1,0:T(8,128)S(1)}, f32[16,384]{1,0:T(8,128)S(1)}, /*index=5*/f32[32,8,128]{2,1,0:T(8,128)}) custom-call(s32[1]{0:T(128)} %bitcast.me, f32[48,16]{1,0:T(8,128)S(1)} %get-tuple-element.46.near, bf16[768,768]{1,0:T(8,128)(2,1)S(1)} %get-tuple-element.38.high, ...), custom_call_target="tpu_custom_call" | custom-call | tf_op jit(solution)/shard_map/direction/pallas_call | solution.py:392
  37.1 2.6 %all-to-all-start.2 = ((f32[32,8,128]{2,1,0:T(8,128)}), f32[32,8,128]{2,1,0:T(8,128)S(1)}, u32[]{:S(2)}, u32[]{:S(2)}) async-start(f32[32,8,128]{2,1,0:T(8,128)} %get-tuple-element.53), calls=%async_computation.2 | async-start | bytes 262144 | tf_op jit(solution)/shard_map/all_to_all | solution.py:418
  39.7 1.7 %collective-permute-start.4 = (f32[16,384]{1,0:T(8,128)S(1)}, f32[16,384]{1,0:T(8,128)S(1)}, u32[]{:S(2)}, u32[]{:S(2)}) collective-permute-start(f32[16,384]{1,0:T(8,128)S(1)} %get-tuple-element.58), channel_id=1, source_target_pairs={{0,4},{1,5},{2,6},{3,7},{4,0},{5,1},{6,2},{7,3},{8,12},{9,13},{10,... | collective-permute-start | bytes 73736 | tf_op jit(solution)/shard_map/ppermute | solution.py:414
  41.4 0.0 collective-permute-start.5
  41.4 6.5 %all-to-all-done.2 = f32[32,8,128]{2,1,0:T(8,128)S(1)} async-done(((f32[32,8,128]{2,1,0:T(8,128)}), f32[32,8,128]{2,1,0:T(8,128)S(1)}, u32[]{:S(2)}, u32[]{:S(2)}) %all-to-all-start.2) | async-done | bytes 131104 | tf_op jit(solution)/shard_map/all_to_all | solution.py:418
  47.9 1.8 %project_image.1 = (f32[48,16]{1,0:T(8,128)S(1)}, f32[16,16]{1,0:T(8,128)S(1)}) custom-call(s32[1]{0:T(128)} %bitcast.me, f32[256,128]{1,0:T(8,128)S(1)} %bitcast.21, f32[256,128]{1,0:T(8,128)S(1)} %bitcast.20, f32[256,256]{1,0:T(8,128)S(1)} %bitcast.15), custom_call_target="tpu_custom_call" | custom-call | tf_op jit(solution)/shard_map/project_image/pallas_call | solution.py:392
  49.7 0.0 collective-permute-done.4.even_got
  49.7 0.0 collective-permute-done.5.odd_got
  49.7 1.8 %second.1 = (f32[16,384]{1,0:T(8,128)S(1)}, f32[16,384]{1,0:T(8,128)S(1)}, f32[16,384]{1,0:T(8,128)S(1)}, f32[16,384]{1,0:T(8,128)S(1)}, f32[16,384]{1,0:T(8,128)S(1)}, /*index=5*/f32[32,16,128]{2,1,0:T(8,128)}) custom-call(s32[1]{0:T(128)} %bitcast.me, f32[48,16]{1,0:T(8,128)S(1)} %get-tuple-element.54.near, bf16[768,768]{1,0:T(8,128)(2,1)S(1)} %get-tuple-element.38.high, ...), custom_call_target="tpu_custom_call" | custom-call | tf_op jit(solution)/shard_map/second/pallas_call | solution.py:392
  51.5 2.6 %all-to-all-start.3 = ((f32[32,16,128]{2,1,0:T(8,128)}), f32[32,16,128]{2,1,0:T(8,128)S(1)}, u32[]{:S(2)}, u32[]{:S(2)}) async-start(f32[32,16,128]{2,1,0:T(8,128)} %get-tuple-element.60), calls=%async_computation.3 | async-start | bytes 524288 | tf_op jit(solution)/shard_map/all_to_all | solution.py:418
  54.1 1.7 %collective-permute-start.6 = (f32[16,384]{1,0:T(8,128)S(1)}, f32[16,384]{1,0:T(8,128)S(1)}, u32[]{:S(2)}, u32[]{:S(2)}) collective-permute-start(f32[16,384]{1,0:T(8,128)S(1)} %get-tuple-element.66), channel_id=1, source_target_pairs={{0,4},{1,5},{2,6},{3,7},{4,0},{5,1},{6,2},{7,3},{8,12},{9,13},{10,... | collective-permute-start | bytes 73736 | tf_op jit(solution)/shard_map/ppermute | solution.py:414
  55.8 1.3 %invert.1.inverse = f32[16,16]{1,0:T(8,128)S(1)} custom-call(f32[16,16]{1,0:T(8,128)S(1)} %get-tuple-element.61.curvature), custom_call_target="tpu_custom_call" | custom-call | tf_op jit(solution)/shard_map/invert/pallas_call | solution.py:392
  57.1 7.5 %all-to-all-done.3.gathered = f32[32,16,128]{2,1,0:T(8,128)S(1)} async-done(((f32[32,16,128]{2,1,0:T(8,128)}), f32[32,16,128]{2,1,0:T(8,128)S(1)}, u32[]{:S(2)}, u32[]{:S(2)}) %all-to-all-start.3) | async-done | bytes 262176 | tf_op jit(solution)/shard_map/all_to_all | solution.py:418
  64.7 2.7 %step.1.steps = f32[48,16]{1,0:T(8,128)S(1)} custom-call(s32[1]{0:T(128)} %bitcast.me, f32[32,16,128]{2,1,0:T(8,128)S(1)} %all-to-all-done.3.gathered, f32[256,256]{1,0:T(8,128)S(1)} %bitcast.16, f32[16,16]{1,0:T(8,128)S(1)} %invert.1.inverse), custom_call_target="tpu_custom_call" | custom-call | tf_op jit(solution)/shard_map/step/pallas_call | solution.py:392
  67.4 1.0 %finish.1 = (f32[16,384]{1,0:T(8,128)}, f32[16,384]{1,0:T(8,128)}) custom-call(s32[1]{0:T(128)} %bitcast.me, f32[48,16]{1,0:T(8,128)S(1)} %step.1.steps, f32[24,768]{1,0:T(8,128)S(1)} %get-tuple-element.47.frame, f32[16,384]{1,0:T(8,128)S(1)} %get-tuple-element.62.start, f32[16,768]{1,0:T(8,128)S(1)} %get-tuple-element.55.search, ...), custom_call_target="tpu_custom_call" | custom-call | tf_op jit(solution)/shard_map/finish/pallas_call | solution.py:392
  (11 shorter events, 0.0 us)
Async XLA Ops:
  3.2 16.0 %all-to-all-start = ((f32[32,1,1280]{2,1,0:T(1,128)}), f32[32,1,1280]{2,1,0:T(1,128)S(1)}, u32[]{:S(2)}, u32[]{:S(2)}) async-start(f32[32,1,1280]{2,1,0:T(1,128)} %get-tuple-element.36), calls=%async_computation | async-start | bytes 327680 | tf_op jit(solution)/shard_map/all_to_all | solution.py:418
  10.6 9.3 %collective-permute-start = (f32[32,384]{1,0:T(8,128)}, f32[32,384]{1,0:T(8,128)S(1)}, u32[]{:S(2)}, u32[]{:S(2)}) collective-permute-start(f32[32,384]{1,0:T(8,128)} %get-tuple-element.42), channel_id=1, source_target_pairs={{0,4},{1,5},{2,6},{3,7},{4,0},{5,1},{6,2},{7,3},{8,12},{9,13},{10,... | collective-permute-start | bytes 147464 | tf_op jit(solution)/shard_map/ppermute | solution.py:414
  12.4 7.5 %collective-permute-start.1 = (f32[32,384]{1,0:T(8,128)}, f32[32,384]{1,0:T(8,128)S(1)}, u32[]{:S(2)}, u32[]{:S(2)}) collective-permute-start(f32[32,384]{1,0:T(8,128)} %get-tuple-element.43), channel_id=1, source_target_pairs={{0,1},{1,0},{2,3},{3,2},{4,8},{5,9},{6,10},{7,11},{8,4},{9,5},{10,... | collective-permute-start | bytes 147464 | tf_op jit(solution)/shard_map/ppermute | solution.py:414
  12.4 1.7 %copy-start = (f32[1,1,768,768]{3,2,1,0:T(8,128)S(1)}, f32[1,1,768,768]{3,2,1,0:T(8,128)}, u32[]{:S(2)}) copy-start(f32[1,1,768,768]{3,2,1,0:T(8,128)} %param.9) | copy-start | bytes 7077892
  14.1 0.7 copy-start.3
  14.8 5.1 %copy-start.1 = (f32[32,384]{1,0:T(8,128)S(1)}, f32[32,384]{1,0:T(8,128)}, u32[]{:S(2)}) copy-start(f32[32,384]{1,0:T(8,128)} %get-tuple-element.41.own) | copy-start | bytes 147460
  14.8 5.2 %copy-start.2 = (f32[8,768]{1,0:T(8,128)S(1)}, f32[8,768]{1,0:T(8,128)}, u32[]{:S(2)}) copy-start(f32[8,768]{1,0:T(8,128)} %get-tuple-element.40.basis) | copy-start | bytes 73732
  21.8 11.5 %all-to-all-start.1 = ((f32[32,8,128]{2,1,0:T(8,128)}), f32[32,8,128]{2,1,0:T(8,128)S(1)}, u32[]{:S(2)}, u32[]{:S(2)}) async-start(f32[32,8,128]{2,1,0:T(8,128)} %get-tuple-element.44), calls=%async_computation.1 | async-start | bytes 262144 | tf_op jit(solution)/shard_map/all_to_all | solution.py:418
  25.1 10.2 %collective-permute-start.2 = (f32[16,384]{1,0:T(8,128)S(1)}, f32[16,384]{1,0:T(8,128)S(1)}, u32[]{:S(2)}, u32[]{:S(2)}) collective-permute-start(f32[16,384]{1,0:T(8,128)S(1)} %get-tuple-element.51), channel_id=1, source_target_pairs={{0,4},{1,5},{2,6},{3,7},{4,0},{5,1},{6,2},{7,3},{8,12},{9,13},{10,... | collective-permute-start | bytes 73736 | tf_op jit(solution)/shard_map/ppermute | solution.py:414
  26.9 8.3 %collective-permute-start.3 = (f32[16,384]{1,0:T(8,128)S(1)}, f32[16,384]{1,0:T(8,128)S(1)}, u32[]{:S(2)}, u32[]{:S(2)}) collective-permute-start(f32[16,384]{1,0:T(8,128)S(1)} %get-tuple-element.52), channel_id=1, source_target_pairs={{0,1},{1,0},{2,3},{3,2},{4,8},{5,9},{6,10},{7,11},{8,4},{9,5},{10,... | collective-permute-start | bytes 73736 | tf_op jit(solution)/shard_map/ppermute | solution.py:414
  37.1 10.8 %all-to-all-start.2 = ((f32[32,8,128]{2,1,0:T(8,128)}), f32[32,8,128]{2,1,0:T(8,128)S(1)}, u32[]{:S(2)}, u32[]{:S(2)}) async-start(f32[32,8,128]{2,1,0:T(8,128)} %get-tuple-element.53), calls=%async_computation.2 | async-start | bytes 262144 | tf_op jit(solution)/shard_map/all_to_all | solution.py:418
  39.7 10.0 %collective-permute-start.4 = (f32[16,384]{1,0:T(8,128)S(1)}, f32[16,384]{1,0:T(8,128)S(1)}, u32[]{:S(2)}, u32[]{:S(2)}) collective-permute-start(f32[16,384]{1,0:T(8,128)S(1)} %get-tuple-element.58), channel_id=1, source_target_pairs={{0,4},{1,5},{2,6},{3,7},{4,0},{5,1},{6,2},{7,3},{8,12},{9,13},{10,... | collective-permute-start | bytes 73736 | tf_op jit(solution)/shard_map/ppermute | solution.py:414
  41.4 8.3 %collective-permute-start.5 = (f32[16,384]{1,0:T(8,128)S(1)}, f32[16,384]{1,0:T(8,128)S(1)}, u32[]{:S(2)}, u32[]{:S(2)}) collective-permute-start(f32[16,384]{1,0:T(8,128)S(1)} %get-tuple-element.59), channel_id=1, source_target_pairs={{0,1},{1,0},{2,3},{3,2},{4,8},{5,9},{6,10},{7,11},{8,4},{9,5},{10,... | collective-permute-start | bytes 73736 | tf_op jit(solution)/shard_map/ppermute | solution.py:414
  51.5 13.2 %all-to-all-start.3 = ((f32[32,16,128]{2,1,0:T(8,128)}), f32[32,16,128]{2,1,0:T(8,128)S(1)}, u32[]{:S(2)}, u32[]{:S(2)}) async-start(f32[32,16,128]{2,1,0:T(8,128)} %get-tuple-element.60), calls=%async_computation.3 | async-start | bytes 524288 | tf_op jit(solution)/shard_map/all_to_all | solution.py:418
  54.1 13.3 %collective-permute-start.6 = (f32[16,384]{1,0:T(8,128)S(1)}, f32[16,384]{1,0:T(8,128)S(1)}, u32[]{:S(2)}, u32[]{:S(2)}) collective-permute-start(f32[16,384]{1,0:T(8,128)S(1)} %get-tuple-element.66), channel_id=1, source_target_pairs={{0,4},{1,5},{2,6},{3,7},{4,0},{5,1},{6,2},{7,3},{8,12},{9,13},{10,... | collective-permute-start | bytes 73736 | tf_op jit(solution)/shard_map/ppermute | solution.py:414
  55.8 11.6 %collective-permute-start.7 = (f32[16,384]{1,0:T(8,128)S(1)}, f32[16,384]{1,0:T(8,128)S(1)}, u32[]{:S(2)}, u32[]{:S(2)}) collective-permute-start(f32[16,384]{1,0:T(8,128)S(1)} %get-tuple-element.67), channel_id=1, source_target_pairs={{0,1},{1,0},{2,3},{3,2},{4,8},{5,9},{6,10},{7,11},{8,4},{9,5},{10,... | collective-permute-start | bytes 73736 | tf_op jit(solution)/shard_map/ppermute | solution.py:414

commit v4 on v3

--- a/solution.py
+++ b/solution.py
@@ -179,7 +179,40 @@
     return [tall[b * PAD : (b + 1) * PAD] for b in range(blocks)]
 
 
-def load_kernel(me, gathered, near, rows, packed, padded, *, stride, k):
+def frame_kernel(
+    me, high, low, basis, own, even_got, odd_got,
+    frame, lifted_rhs, lifted_scale, applied, mine, scaled, *, subs, chain,
+):
+    face = own.shape[1]
+    cases = lifted_rhs.shape[0]
+    from_left, from_right = join_sides(me[0], subs, chain, even_got[...], odd_got[...])
+    zero = jnp.zeros((PAD, face), f32)
+    v = jnp.concatenate(
+        [
+            jnp.concatenate([from_left[:PAD], zero], axis=1),
+            basis[...],
+            jnp.concatenate([zero, from_right[:PAD]], axis=1),
+        ],
+        axis=0,
+    )
+    both = jnp.concatenate([from_left, own[...]], axis=1)
+    lb = both[PAD : PAD + cases]
+    ld = both[PAD + cases : PAD + cases + 1]
+    frame[: 3 * PAD] = v
+    frame[3 * PAD :] = v * ld
+    lifted_rhs[...] = lb
+    lifted_scale[...] = ld
+    applied[...] = times_schur(v, high, low)
+    bd = basis[...] * ld
+    mine[...] = nt(jnp.concatenate([basis[...], bd], axis=0), lb)
+    scaled[...] = nt(bd, v)
+
+
+def start_kernel(
+    me, gathered, frame, applied, mine, scaled,
+    start, image_out, to_even, to_odd, rows, payload, packed, padded, *, subs, stride, k,
+):
+    face = start.shape[1]
     nc, cases = packed.shape
     each = nc + cases
     peers = gathered.shape[0]
@@ -189,62 +222,47 @@
     for i in range(peers):
         packed[i * k : (i + 1) * k] = rows[i, :k, nc:each]
     table = rows[:, :, :nc].reshape(peers * PAD, nc)
-    near[...] = near_blocks(nn(table, packed[...]), padded, me[0], stride)
-
-
-def start_kernel(
-    me, near, high, low, basis, own, even_got, odd_got,
-    frame, lifted_rhs, lifted_scale, start, image_out, to_even, to_odd, payload, *, subs, chain,
-):
-    face = own.shape[1]
-    cases = near.shape[1]
-    from_left, from_right = join_sides(me[0], subs, chain, even_got[...], odd_got[...])
-    zero = jnp.zeros((PAD, face), f32)
-    v = jnp.concatenate(
-        [
-            jnp.concatenate([from_left[:PAD], zero], axis=1),
-            basis[...],
-            jnp.concatenate([zero, from_right[:PAD]], axis=1),
-        ],
-        axis=0,
-    )
-    frame[...] = v
-    both = jnp.concatenate([from_left, own[...]], axis=1)
-    lb = both[PAD : PAD + cases]
-    ld = both[PAD + cases : PAD + cases + 1]
-    lifted_rhs[...] = lb
-    lifted_scale[...] = ld
-    m0 = tn(near[...], v)
-    start[...] = m0[:, face:]
-    image = times_schur(m0, high, low)
+    near = near_blocks(nn(table, packed[...]), padded, me[0], stride)
+    start[...] = tn(near, frame[: 3 * PAD, face:])
+    image = tn(near, applied[...])
     image_out[...] = image
     to_even[...], to_odd[...] = split_sides(me[0], subs, image[:, face:], image[:, :face])
-    shares = -nt(jnp.concatenate([v, v * ld], axis=0), image)
-    mine = nt(jnp.concatenate([basis[...], basis[...] * ld], axis=0), lb)
-    scaled = nt(basis[...] * ld, v)
-    part = side_by_side(shares, 6)
+    part = side_by_side(-nt(frame[...], image), 6)
     part[1] = part[1] + mine[:PAD]
     part[4] = part[4] + mine[PAD:]
     used = 6 * cases + 3 * PAD
-    width = payload.shape[2]
-    row = jnp.concatenate(part + [scaled, jnp.zeros((PAD, width - used), f32)], axis=1)
-    payload[...] = jnp.broadcast_to(row[None], payload.shape)
-
-
-def project_kernel(me, gathered, scaled, coarse, near, curvature, packed, padded, *, stride, k, total):
+    width = payload.shape[2] // k
+    row = jnp.concatenate(part + [scaled[...], jnp.zeros((PAD, width - used), f32)], axis=1)
+    line = jnp.concatenate([row[i : i + 1] for i in range(k)], axis=1)
+    payload[...] = jnp.broadcast_to(line[None], payload.shape)
+
+
+def project_first_kernel(me, gathered, coarse, near, unfolded, packed, padded, *, stride, k):
     nc, cases = packed.shape
-    wide = gathered[...]
+    peers, _, width = unfolded.shape
+    unfolded[...] = jnp.zeros_like(unfolded)
+    for i in range(k):
+        unfolded[:, i, :] = gathered[:, 0, i * width : (i + 1) * width]
+    wide = unfolded[...].reshape(peers * PAD, width)
+    project(me, wide, wide, coarse, near, packed, padded, nc, cases, stride, k)
+
+
+def project(me, wide, scaled, coarse, near, packed, padded, nc, cases, stride, k):
     g = gather_sum(wide, 0, cases, stride)
     h = gather_sum(wide, 3 * cases, cases, stride)
     c1 = coarse_times(coarse, nc, g, packed, k)
     c2 = coarse_times(
-        coarse, nc, h - scaled_gram_times(scaled[...], 6 * cases, c1, k, stride // PAD), packed, k
+        coarse, nc, h - scaled_gram_times(scaled, 6 * cases, c1, k, stride // PAD), packed, k
     )
     near[: 3 * PAD] = near_blocks(c1, padded, me[0], stride)
     near[3 * PAD :] = near_blocks(c2, padded, me[0], stride)
-    if not total:
-        curvature[...] = jnp.zeros_like(curvature)
-    for b in range(cases // PAD if total else 0):
+
+
+def project_kernel(me, gathered, scaled, coarse, near, curvature, packed, padded, *, stride, k):
+    nc, cases = packed.shape
+    wide = gathered[...]
+    project(me, wide, scaled[...], coarse, near, packed, padded, nc, cases, stride, k)
+    for b in range(cases // PAD):
         piece = wide[:, (6 + b) * cases : (7 + b) * cases]
         curvature[b * PAD : (b + 1) * PAD] = piece.reshape(-1, PAD, cases).sum(axis=0)
 
@@ -256,7 +274,7 @@
     cases, face = even_got.shape
     from_left, from_right = join_sides(me[0], subs, chain, even_got[...], odd_got[...])
     moved = image_in[...] + jnp.concatenate([from_left, from_right], axis=1)
-    v = frame[...]
+    v = frame[: 3 * PAD]
     r = lifted_rhs[...] - moved - tn(near[: 3 * PAD], v)
     s = lifted_scale[...] * r - tn(near[3 * PAD :], v)
     search[...] = s
@@ -264,7 +282,7 @@
     image = times_schur(s, high, low)
     image_out[...] = image
     to_even[...], to_odd[...] = split_sides(me[0], subs, image[:, face:], image[:, :face])
-    shares = nt(jnp.concatenate([v, v * lifted_scale[...]], axis=0), image)
+    shares = nt(frame[...], image)
     energy = nt(s, image)
     part = side_by_side(shares, 6) + side_by_side(energy, cases // PAD)
     used = (6 + cases // PAD) * cases
@@ -281,7 +299,7 @@
     cases, face = even_got.shape
     from_left, from_right = join_sides(me[0], subs, chain, even_got[...], odd_got[...])
     q = image_in[...] + jnp.concatenate([from_left, from_right], axis=1)
-    v = frame[...]
+    v = frame[: 3 * PAD]
     p = q - tn(near[: 3 * PAD], v)
     z = lifted_scale[...] * p - tn(near[3 * PAD :], v)
     projected[...] = p[:, face:]
@@ -465,33 +483,35 @@
         [((size, size), bf16), ((size, size), bf16)],
         "permute",
     )
-    near, coarse_rows = call(
-        head(load_kernel, **grid),
-        (me, shared),
-        [((3 * PAD, cases), f32), ((peers, PAD, wide0), f32)],
-        "load",
-        scratch=work,
-    )
-    coarse_rows = coarse_rows.reshape(rows, wide0)
-
-    frame, lifted_rhs, lifted_scale, start, image, to_even, to_odd, payload = call(
-        head(start_kernel, **line),
-        (me, near, high, low, basis, own, *got),
+    frame, lifted_rhs, lifted_scale, applied, mine, scaled = call(
+        head(frame_kernel, **line),
+        (me, high, low, basis, own, *got),
         [
-            ((3 * PAD, size), f32), (lifted, f32), ((1, size), f32), (vec, f32), (lifted, f32),
-            (vec, f32), (vec, f32), ((peers, PAD, wide1), f32),
+            ((6 * PAD, size), f32), (lifted, f32), ((1, size), f32), ((3 * PAD, size), f32),
+            ((2 * PAD, cases), f32), ((PAD, 3 * PAD), f32),
+        ],
+        "frame",
+    )
+    start, image, to_even, to_odd, coarse_rows, payload = call(
+        head(start_kernel, subs=subs, **grid),
+        (me, shared, frame, applied, mine, scaled),
+        [
+            (vec, f32), (lifted, f32), (vec, f32), (vec, f32), ((peers, PAD, wide0), f32),
+            ((peers, 1, k * wide1), f32),
         ],
         "start",
-    )
+        scratch=work,
+    )
+    coarse_rows = coarse_rows.reshape(rows, wide0)
     got = exchange(to_even, to_odd)
-    first = spread(payload).reshape(rows, wide1)
-    near, _ = call(
-        head(project_kernel, total=False, **grid),
-        (me, first, first, coarse_rows),
-        [((6 * PAD, cases), f32), (small, f32)],
+    near, first = call(
+        head(project_first_kernel, **grid),
+        (me, spread(payload), coarse_rows),
+        [((6 * PAD, cases), f32), ((peers, PAD, wide1), f32)],
         "project_start",
         scratch=work,
     )
+    first = first.reshape(rows, wide1)
 
     search, residual, image, to_even, to_odd, payload = call(
         head(direction_kernel, **line),
@@ -502,7 +522,7 @@
     got = exchange(to_even, to_odd)
     shared = spread(payload).reshape(rows, wide2)
     near, curvature = call(
-        head(project_kernel, total=True, **grid),
+        head(project_kernel, **grid),
         (me, shared, first, coarse_rows),
         [((6 * PAD, cases), f32), (small, f32)],
         "project_image",

time: 68.9 us -> 68.7 us (level)
  waiting for transfers between devices: 23.2 us -> 22.1 us
  starting transfers between devices: 22.9 us -> 23.6 us
    all_to_all x4, waiting for transfers between devices: 23.2 us -> 22.1 us  [spread(): return lax.all_to_all(payload, AXES, 0, 0)]
    all_to_all x4, starting transfers between devices: 15.8 us -> 16.5 us  [spread(): return lax.all_to_all(payload, AXES, 0, 0)]
where the time goes in v4:
time: 68.7 us; the launch traced here: 68.3 us
  starting transfers between devices  23.6 us (34%)
  waiting for transfers between devices  22.1 us (32%)
  Pallas kernels  18.8 us (27%)
  local copies, waits for them, and re-layouts  2.35 us (3%)
  between operations  1.43 us (2%)
    all_to_all x4, waiting for transfers between devices, spread(): return lax.all_to_all(payload, AXES, 0, 0)  22.1 us
    pallas_call x11, Pallas kernels, call(): pl.pallas_call(kernel, out_shape=[jax.ShapeDtypeStruct(s, d) for s, d in...  18.8 us
    all_to_all x4, starting transfers between devices, spread(): return lax.all_to_all(payload, AXES, 0, 0)  16.5 us
    ppermute x8, starting transfers between devices, exchange(): return (lax.ppermute(to_even, AXES, even), lax.ppermute(to_odd, AXES, odd))  7.11 us
    unnamed x8, local copies, waits for them, and re-layouts  2.35 us
  transfers between devices with their start and end apart: 12, of which 4 were waited for; matrix products, arithmetic and copies ran while one was open for 0% of the time, Pallas kernels for 15%

profile of v4, /device:TPU:0, one launch (start us, length us, event | category | flops | bytes accessed | tf_op | source)
XLA Modules:
  0.0 68.3 jit_solution(7814981114892804834)
XLA Ops:
  1.3 1.9 %pack.1 = (f32[8,768]{1,0:T(8,128)}, f32[32,384]{1,0:T(8,128)}, f32[32,384]{1,0:T(8,128)}, f32[32,384]{1,0:T(8,128)}, f32[32,1,1280]{2,1,0:T(1,128)}) custom-call(s32[1]{0:T(128)} %bitcast.me, s32[1]{0:T(128)} %bitcast.13.count, f32[6,1,768]{2,1,0:T(1,128)} %bitcast.23, s32[1,384]{1,0:T(1,128)} %bitcast.20, f32[6,1,16]{2,1,0:T(1,128)} %bitcast.24, ...), custom_call_target="tpu_custom_call" | custom-call | tf_op jit(solution)/shard_map/pack/pallas_call | solution.py:410
  3.2 7.3 %all-to-all-start = ((f32[32,1,1280]{2,1,0:T(1,128)}), f32[32,1,1280]{2,1,0:T(1,128)S(1)}, u32[]{:S(2)}, u32[]{:S(2)}) async-start(f32[32,1,1280]{2,1,0:T(1,128)} %get-tuple-element.39), calls=%async_computation | async-start | bytes 327680 | tf_op jit(solution)/shard_map/all_to_all | solution.py:436
  10.6 1.8 %collective-permute-start = (f32[32,384]{1,0:T(8,128)}, f32[32,384]{1,0:T(8,128)S(1)}, u32[]{:S(2)}, u32[]{:S(2)}) collective-permute-start(f32[32,384]{1,0:T(8,128)} %get-tuple-element.44), channel_id=1, source_target_pairs={{0,4},{1,5},{2,6},{3,7},{4,0},{5,1},{6,2},{7,3},{8,12},{9,13},{10,... | collective-permute-start | bytes 147464 | tf_op jit(solution)/shard_map/ppermute | solution.py:432
  12.4 0.0 collective-permute-start.1
  12.4 1.7 %copy-done = f32[1,1,768,768]{3,2,1,0:T(8,128)S(1)} copy-done((f32[1,1,768,768]{3,2,1,0:T(8,128)S(1)}, f32[1,1,768,768]{3,2,1,0:T(8,128)}, u32[]{:S(2)}) %copy-start) | copy-done | bytes 2359320
  14.1 0.7 copy-done.3
  14.8 1.6 %permute.1 = (bf16[768,768]{1,0:T(8,128)(2,1)S(1)}, bf16[768,768]{1,0:T(8,128)(2,1)S(1)}) custom-call(s32[1]{0:T(128)} %bitcast.me, s32[1,384]{1,0:T(1,128)S(1)} %bitcast.21, f32[768,768]{1,0:T(8,128)S(1)} %bitcast.17), custom_call_target="tpu_custom_call" | custom-call | tf_op jit(solution)/shard_map/permute/pallas_call | solution.py:410
  16.4 0.0 collective-permute-done.1.odd_got
  16.4 0.7 frame.1
  17.1 2.1 %all-to-all-done.gathered = f32[32,1,1280]{2,1,0:T(1,128)S(1)} async-done(((f32[32,1,1280]{2,1,0:T(1,128)}), f32[32,1,1280]{2,1,0:T(1,128)S(1)}, u32[]{:S(2)}, u32[]{:S(2)}) %all-to-all-start) | async-done | bytes 163872 | tf_op jit(solution)/shard_map/all_to_all | solution.py:436
  19.2 2.3 %start.1 = (f32[16,384]{1,0:T(8,128)S(1)}, f32[16,768]{1,0:T(8,128)S(1)}, f32[16,384]{1,0:T(8,128)S(1)}, f32[16,384]{1,0:T(8,128)S(1)}, f32[32,8,256]{2,1,0:T(8,128)S(1)}, /*index=5*/f32[32,1,768]{2,1,0:T(1,128)}) custom-call(s32[1]{0:T(128)} %bitcast.me, f32[32,1,1280]{2,1,0:T(1,128)S(1)} %all-to-all-done.gathered, f32[48,768]{1,0:T(8,128)S(1)} %get-tuple-element.46.frame, ...), custom_call_target="tpu_custom_call" | custom-call | tf_op jit(solution)/shard_map/start/pallas_call | solution.py:410
  21.4 4.0 %all-to-all-start.1 = ((f32[32,1,768]{2,1,0:T(1,128)}), f32[32,1,768]{2,1,0:T(1,128)S(1)}, u32[]{:S(2)}, u32[]{:S(2)}) async-start(f32[32,1,768]{2,1,0:T(1,128)} %get-tuple-element.50), calls=%async_computation.1 | async-start | bytes 196608 | tf_op jit(solution)/shard_map/all_to_all | solution.py:436
  25.4 1.8 %collective-permute-start.2 = (f32[16,384]{1,0:T(8,128)S(1)}, f32[16,384]{1,0:T(8,128)S(1)}, u32[]{:S(2)}, u32[]{:S(2)}) collective-permute-start(f32[16,384]{1,0:T(8,128)S(1)} %get-tuple-element.56), channel_id=1, source_target_pairs={{0,4},{1,5},{2,6},{3,7},{4,0},{5,1},{6,2},{7,3},{8,12},{9,13},{10,... | collective-permute-start | bytes 73736 | tf_op jit(solution)/shard_map/ppermute | solution.py:432
  27.3 5.9 %all-to-all-done.1.gathered = f32[32,1,768]{2,1,0:T(1,128)S(1)} async-done(((f32[32,1,768]{2,1,0:T(1,128)}), f32[32,1,768]{2,1,0:T(1,128)S(1)}, u32[]{:S(2)}, u32[]{:S(2)}) %all-to-all-start.1) | async-done | bytes 98336 | tf_op jit(solution)/shard_map/all_to_all | solution.py:436
  33.2 1.8 %project_start.1 = (f32[48,16]{1,0:T(8,128)S(1)}, f32[32,8,128]{2,1,0:T(8,128)S(1)}) custom-call(s32[1]{0:T(128)} %bitcast.me, f32[32,1,768]{2,1,0:T(1,128)S(1)} %all-to-all-done.1.gathered, f32[256,256]{1,0:T(8,128)S(1)} %bitcast.14), custom_call_target="tpu_custom_call" | custom-call | tf_op jit(solution)/shard_map/project_start/pallas_call | solution.py:410
  35.1 0.0 collective-permute-done.2.even_got
  35.1 0.0 collective-permute-done.3.odd_got
  35.1 1.8 %direction.1 = (f32[16,768]{1,0:T(8,128)S(1)}, f32[16,384]{1,0:T(8,128)S(1)}, f32[16,768]{1,0:T(8,128)S(1)}, f32[16,384]{1,0:T(8,128)S(1)}, f32[16,384]{1,0:T(8,128)S(1)}, /*index=5*/f32[32,8,128]{2,1,0:T(8,128)}) custom-call(s32[1]{0:T(128)} %bitcast.me, f32[48,16]{1,0:T(8,128)S(1)} %get-tuple-element.52.near, bf16[768,768]{1,0:T(8,128)(2,1)S(1)} %get-tuple-element.40.high, ...), custom_call_target="tpu_custom_call" | custom-call | tf_op jit(solution)/shard_map/direction/pallas_call | solution.py:410
  36.9 2.6 %all-to-all-start.2 = ((f32[32,8,128]{2,1,0:T(8,128)}), f32[32,8,128]{2,1,0:T(8,128)S(1)}, u32[]{:S(2)}, u32[]{:S(2)}) async-start(f32[32,8,128]{2,1,0:T(8,128)} %get-tuple-element.58), calls=%async_computation.2 | async-start | bytes 262144 | tf_op jit(solution)/shard_map/all_to_all | solution.py:436
  39.5 1.7 %collective-permute-start.4 = (f32[16,384]{1,0:T(8,128)S(1)}, f32[16,384]{1,0:T(8,128)S(1)}, u32[]{:S(2)}, u32[]{:S(2)}) collective-permute-start(f32[16,384]{1,0:T(8,128)S(1)} %get-tuple-element.64), channel_id=1, source_target_pairs={{0,4},{1,5},{2,6},{3,7},{4,0},{5,1},{6,2},{7,3},{8,12},{9,13},{10,... | collective-permute-start | bytes 73736 | tf_op jit(solution)/shard_map/ppermute | solution.py:432
  41.2 0.0 collective-permute-start.5
  41.2 6.5 %all-to-all-done.2 = f32[32,8,128]{2,1,0:T(8,128)S(1)} async-done(((f32[32,8,128]{2,1,0:T(8,128)}), f32[32,8,128]{2,1,0:T(8,128)S(1)}, u32[]{:S(2)}, u32[]{:S(2)}) %all-to-all-start.2) | async-done | bytes 131104 | tf_op jit(solution)/shard_map/all_to_all | solution.py:436
  47.7 1.8 %project_image.1 = (f32[48,16]{1,0:T(8,128)S(1)}, f32[16,16]{1,0:T(8,128)S(1)}) custom-call(s32[1]{0:T(128)} %bitcast.me, f32[256,128]{1,0:T(8,128)S(1)} %bitcast.18, f32[256,128]{1,0:T(8,128)S(1)} %bitcast.19, f32[256,256]{1,0:T(8,128)S(1)} %bitcast.15), custom_call_target="tpu_custom_call" | custom-call | tf_op jit(solution)/shard_map/project_image/pallas_call | solution.py:410
  49.5 0.0 collective-permute-done.5.odd_got
  49.5 1.8 %second.1 = (f32[16,384]{1,0:T(8,128)S(1)}, f32[16,384]{1,0:T(8,128)S(1)}, f32[16,384]{1,0:T(8,128)S(1)}, f32[16,384]{1,0:T(8,128)S(1)}, f32[16,384]{1,0:T(8,128)S(1)}, /*index=5*/f32[32,16,128]{2,1,0:T(8,128)}) custom-call(s32[1]{0:T(128)} %bitcast.me, f32[48,16]{1,0:T(8,128)S(1)} %get-tuple-element.60.near, bf16[768,768]{1,0:T(8,128)(2,1)S(1)} %get-tuple-element.40.high, ...), custom_call_target="tpu_custom_call" | custom-call | tf_op jit(solution)/shard_map/second/pallas_call | solution.py:410
  51.3 2.6 %all-to-all-start.3 = ((f32[32,16,128]{2,1,0:T(8,128)}), f32[32,16,128]{2,1,0:T(8,128)S(1)}, u32[]{:S(2)}, u32[]{:S(2)}) async-start(f32[32,16,128]{2,1,0:T(8,128)} %get-tuple-element.66), calls=%async_computation.3 | async-start | bytes 524288 | tf_op jit(solution)/shard_map/all_to_all | solution.py:436
  53.9 1.7 %collective-permute-start.6 = (f32[16,384]{1,0:T(8,128)S(1)}, f32[16,384]{1,0:T(8,128)S(1)}, u32[]{:S(2)}, u32[]{:S(2)}) collective-permute-start(f32[16,384]{1,0:T(8,128)S(1)} %get-tuple-element.72), channel_id=1, source_target_pairs={{0,4},{1,5},{2,6},{3,7},{4,0},{5,1},{6,2},{7,3},{8,12},{9,13},{10,... | collective-permute-start | bytes 73736 | tf_op jit(solution)/shard_map/ppermute | solution.py:432
  55.6 0.0 collective-permute-start.7
  55.6 1.3 %invert.1.inverse = f32[16,16]{1,0:T(8,128)S(1)} custom-call(f32[16,16]{1,0:T(8,128)S(1)} %get-tuple-element.67.curvature), custom_call_target="tpu_custom_call" | custom-call | tf_op jit(solution)/shard_map/invert/pallas_call | solution.py:410
  57.0 7.5 %all-to-all-done.3.gathered = f32[32,16,128]{2,1,0:T(8,128)S(1)} async-done(((f32[32,16,128]{2,1,0:T(8,128)}), f32[32,16,128]{2,1,0:T(8,128)S(1)}, u32[]{:S(2)}, u32[]{:S(2)}) %all-to-all-start.3) | async-done | bytes 262176 | tf_op jit(solution)/shard_map/all_to_all | solution.py:436
  64.5 2.7 %step.1.steps = f32[48,16]{1,0:T(8,128)S(1)} custom-call(s32[1]{0:T(128)} %bitcast.me, f32[32,16,128]{2,1,0:T(8,128)S(1)} %all-to-all-done.3.gathered, f32[256,256]{1,0:T(8,128)S(1)} %bitcast.16, f32[16,16]{1,0:T(8,128)S(1)} %invert.1.inverse), custom_call_target="tpu_custom_call" | custom-call | tf_op jit(solution)/shard_map/step/pallas_call | solution.py:410
  67.2 1.0 %finish.1 = (f32[16,384]{1,0:T(8,128)}, f32[16,384]{1,0:T(8,128)}) custom-call(s32[1]{0:T(128)} %bitcast.me, f32[48,16]{1,0:T(8,128)S(1)} %step.1.steps, f32[48,768]{1,0:T(8,128)S(1)} %get-tuple-element.46.frame, f32[16,384]{1,0:T(8,128)S(1)} %get-tuple-element.68.start, f32[16,768]{1,0:T(8,128)S(1)} %get-tuple-element.61.search, ...), custom_call_target="tpu_custom_call" | custom-call | tf_op jit(solution)/shard_map/finish/pallas_call | solution.py:410
  (11 shorter events, 0.0 us)
Async XLA Ops:
  3.2 16.0 %all-to-all-start = ((f32[32,1,1280]{2,1,0:T(1,128)}), f32[32,1,1280]{2,1,0:T(1,128)S(1)}, u32[]{:S(2)}, u32[]{:S(2)}) async-start(f32[32,1,1280]{2,1,0:T(1,128)} %get-tuple-element.39), calls=%async_computation | async-start | bytes 327680 | tf_op jit(solution)/shard_map/all_to_all | solution.py:436
  10.6 5.8 %collective-permute-start = (f32[32,384]{1,0:T(8,128)}, f32[32,384]{1,0:T(8,128)S(1)}, u32[]{:S(2)}, u32[]{:S(2)}) collective-permute-start(f32[32,384]{1,0:T(8,128)} %get-tuple-element.44), channel_id=1, source_target_pairs={{0,4},{1,5},{2,6},{3,7},{4,0},{5,1},{6,2},{7,3},{8,12},{9,13},{10,... | collective-permute-start | bytes 147464 | tf_op jit(solution)/shard_map/ppermute | solution.py:432
  12.4 4.0 %collective-permute-start.1 = (f32[32,384]{1,0:T(8,128)}, f32[32,384]{1,0:T(8,128)S(1)}, u32[]{:S(2)}, u32[]{:S(2)}) collective-permute-start(f32[32,384]{1,0:T(8,128)} %get-tuple-element.45), channel_id=1, source_target_pairs={{0,1},{1,0},{2,3},{3,2},{4,8},{5,9},{6,10},{7,11},{8,4},{9,5},{10,... | collective-permute-start | bytes 147464 | tf_op jit(solution)/shard_map/ppermute | solution.py:432
  12.4 1.7 %copy-start = (f32[1,1,768,768]{3,2,1,0:T(8,128)S(1)}, f32[1,1,768,768]{3,2,1,0:T(8,128)}, u32[]{:S(2)}) copy-start(f32[1,1,768,768]{3,2,1,0:T(8,128)} %param.9) | copy-start | bytes 7077892
  14.1 0.7 copy-start.3
  14.8 1.6 %copy-start.1 = (f32[32,384]{1,0:T(8,128)S(1)}, f32[32,384]{1,0:T(8,128)}, u32[]{:S(2)}) copy-start(f32[32,384]{1,0:T(8,128)} %get-tuple-element.43.own) | copy-start | bytes 147460
  14.8 1.7 %copy-start.2 = (f32[8,768]{1,0:T(8,128)S(1)}, f32[8,768]{1,0:T(8,128)}, u32[]{:S(2)}) copy-start(f32[8,768]{1,0:T(8,128)} %get-tuple-element.42.basis) | copy-start | bytes 73732
  21.4 11.8 %all-to-all-start.1 = ((f32[32,1,768]{2,1,0:T(1,128)}), f32[32,1,768]{2,1,0:T(1,128)S(1)}, u32[]{:S(2)}, u32[]{:S(2)}) async-start(f32[32,1,768]{2,1,0:T(1,128)} %get-tuple-element.50), calls=%async_computation.1 | async-start | bytes 196608 | tf_op jit(solution)/shard_map/all_to_all | solution.py:436
  25.4 9.6 %collective-permute-start.2 = (f32[16,384]{1,0:T(8,128)S(1)}, f32[16,384]{1,0:T(8,128)S(1)}, u32[]{:S(2)}, u32[]{:S(2)}) collective-permute-start(f32[16,384]{1,0:T(8,128)S(1)} %get-tuple-element.56), channel_id=1, source_target_pairs={{0,4},{1,5},{2,6},{3,7},{4,0},{5,1},{6,2},{7,3},{8,12},{9,13},{10,... | collective-permute-start | bytes 73736 | tf_op jit(solution)/shard_map/ppermute | solution.py:432
  27.3 7.8 %collective-permute-start.3 = (f32[16,384]{1,0:T(8,128)S(1)}, f32[16,384]{1,0:T(8,128)S(1)}, u32[]{:S(2)}, u32[]{:S(2)}) collective-permute-start(f32[16,384]{1,0:T(8,128)S(1)} %get-tuple-element.57), channel_id=1, source_target_pairs={{0,1},{1,0},{2,3},{3,2},{4,8},{5,9},{6,10},{7,11},{8,4},{9,5},{10,... | collective-permute-start | bytes 73736 | tf_op jit(solution)/shard_map/ppermute | solution.py:432
  36.9 10.8 %all-to-all-start.2 = ((f32[32,8,128]{2,1,0:T(8,128)}), f32[32,8,128]{2,1,0:T(8,128)S(1)}, u32[]{:S(2)}, u32[]{:S(2)}) async-start(f32[32,8,128]{2,1,0:T(8,128)} %get-tuple-element.58), calls=%async_computation.2 | async-start | bytes 262144 | tf_op jit(solution)/shard_map/all_to_all | solution.py:436
  39.5 10.0 %collective-permute-start.4 = (f32[16,384]{1,0:T(8,128)S(1)}, f32[16,384]{1,0:T(8,128)S(1)}, u32[]{:S(2)}, u32[]{:S(2)}) collective-permute-start(f32[16,384]{1,0:T(8,128)S(1)} %get-tuple-element.64), channel_id=1, source_target_pairs={{0,4},{1,5},{2,6},{3,7},{4,0},{5,1},{6,2},{7,3},{8,12},{9,13},{10,... | collective-permute-start | bytes 73736 | tf_op jit(solution)/shard_map/ppermute | solution.py:432
  41.2 8.3 %collective-permute-start.5 = (f32[16,384]{1,0:T(8,128)S(1)}, f32[16,384]{1,0:T(8,128)S(1)}, u32[]{:S(2)}, u32[]{:S(2)}) collective-permute-start(f32[16,384]{1,0:T(8,128)S(1)} %get-tuple-element.65), channel_id=1, source_target_pairs={{0,1},{1,0},{2,3},{3,2},{4,8},{5,9},{6,10},{7,11},{8,4},{9,5},{10,... | collective-permute-start | bytes 73736 | tf_op jit(solution)/shard_map/ppermute | solution.py:432
  51.3 13.2 %all-to-all-start.3 = ((f32[32,16,128]{2,1,0:T(8,128)}), f32[32,16,128]{2,1,0:T(8,128)S(1)}, u32[]{:S(2)}, u32[]{:S(2)}) async-start(f32[32,16,128]{2,1,0:T(8,128)} %get-tuple-element.66), calls=%async_computation.3 | async-start | bytes 524288 | tf_op jit(solution)/shard_map/all_to_all | solution.py:436
  53.9 13.3 %collective-permute-start.6 = (f32[16,384]{1,0:T(8,128)S(1)}, f32[16,384]{1,0:T(8,128)S(1)}, u32[]{:S(2)}, u32[]{:S(2)}) collective-permute-start(f32[16,384]{1,0:T(8,128)S(1)} %get-tuple-element.72), channel_id=1, source_target_pairs={{0,4},{1,5},{2,6},{3,7},{4,0},{5,1},{6,2},{7,3},{8,12},{9,13},{10,... | collective-permute-start | bytes 73736 | tf_op jit(solution)/shard_map/ppermute | solution.py:432
  55.6 11.6 %collective-permute-start.7 = (f32[16,384]{1,0:T(8,128)S(1)}, f32[16,384]{1,0:T(8,128)S(1)}, u32[]{:S(2)}, u32[]{:S(2)}) collective-permute-start(f32[16,384]{1,0:T(8,128)S(1)} %get-tuple-element.73), channel_id=1, source_target_pairs={{0,1},{1,0},{2,3},{3,2},{4,8},{5,9},{6,10},{7,11},{8,4},{9,5},{10,... | collective-permute-start | bytes 73736 | tf_op jit(solution)/shard_map/ppermute | solution.py:432
